TPU v7x, 128 devices: a whole 4x4x4 slice. The times are simulated.
128 devices in a mesh: lon: 32 (over x, y, z_hi), lev: 4 (over z_lo, core).
Axes of the slice: x: 4, y: 4, z: 4 (z_hi: 2, z_lo: 2; z = z_hi * 2 + z_lo), core: 2. Of those that a mesh axis runs over, the one named last changes fastest.
Arguments:
- field: float32 [72, 512, 128], P('lev', 'lon'), may hold values from -6 to 6
- ens: bfloat16 [80, 72, 512, 128], P(None, 'lev', 'lon'), may hold values from -2 to 2
- sdev: float32 [72, 512, 128], P('lev', 'lon'), may hold values from 0.5 to 2
- lon_taper: bfloat16 [17], replicated, may hold values from 0 to 0.079589844
- static_taper: bfloat16 [17], replicated, may hold values from 0 to 0.079589844
- loc_vert: bfloat16 [72, 72], P('lev'), may hold values from -0.75 to 0.75
- static_vert: bfloat16 [72, 72], P('lev'), may hold values from -0.75 to 0.75
- obs_block: int32 [32768], P('lon'), may hold values from -1 to 511, as said below
- obs_value: float32 [32768], P('lon'), may hold values from -6 to 6
- obs_rinv: float32 [32768], P('lon'), may hold values from 0.25 to 4
- obs_horiz: float32 [32768, 128], P('lon'), may hold values from -0.5 to 0.5
- obs_vert: float32 [32768, 72], P('lon', 'lev'), may hold values from -0.75 to 0.75
Outputs:
- increment: float32 [72, 512, 128], P('lev', 'lon')
- adjoint_field: float32 [72, 512, 128], P('lev', 'lon')
- obs_cost: float32 [], replicated
Inputs may be any that keep to these rules, and one draw needn't show every extreme that they name: `obs_block`: each longitude sector's 1024 slots name only blocks within that sector's longitudes; live slots come first, in non-falling block order; at least half of a sector's slots are live, and some sector has all its slots live.
All inputs are finite; a program needn't handle non-finite values.
Results may differ from a plain program's by a relative error of at most 0.0041.
Values may be sent and summed in bfloat16 or wider, within the bound.
A program may use at most 128 MiB of HBM per device.

v0:
```python
import jax
import jax.numpy as jnp
from jax import lax
from jax.sharding import PartitionSpec as P

ens_weight = 0.8
static_weight = 0.5


def padded(block, sides, width):
    for axis, dim in sides:
        count = lax.axis_size(axis)
        forward = [(i, i + 1) for i in range(count - 1)]
        forward.append((count - 1, 0))
        backward = [(target, source) for source, target in forward]
        low = lax.ppermute(
            lax.slice_in_dim(block, block.shape[dim] - width, None, axis=dim), axis, forward
        )
        high = lax.ppermute(lax.slice_in_dim(block, 0, width, axis=dim), axis, backward)
        block = jnp.concatenate([low, block, high], axis=dim)
    return block


def side_by_side(arrays, axis, dim, along):
    both = jnp.concatenate(arrays, axis=along)
    whole, at, done = (lax.all_gather(both, axis, axis=dim, tiled=True), 0, [])
    for a in arrays:
        done.append(lax.slice_in_dim(whole, at, at + a.shape[along], axis=along))
        at += a.shape[along]
    return tuple(done)


def sent_together(arrays, axis, split_dim, concat_dim, along):
    both = jnp.concatenate(arrays, axis=along)
    whole, at, done = (
        lax.all_to_all(both, axis, split_axis=split_dim, concat_axis=concat_dim, tiled=True),
        0,
        [],
    )
    for a in arrays:
        done.append(lax.slice_in_dim(whole, at, at + a.shape[along], axis=along))
        at += a.shape[along]
    return tuple(done)


def sent_to_all(x, axis):
    copies = jnp.broadcast_to(x, (lax.axis_size(axis), *x.shape))
    return lax.all_to_all(copies, axis, split_axis=0, concat_axis=0, tiled=True)


def taken_together(x, axis):
    return sent_to_all(x, axis).sum(axis=0)


def band_matrix(taper, columns):
    width = taper.shape[0]
    extended = columns + width - 1
    offsets = jnp.arange(extended)[:, None] - jnp.arange(columns)[None, :]
    onehot = (offsets[:, :, None] == jnp.arange(width)[None, None, :]).astype(jnp.float32)
    return jnp.einsum("eid,d->ei", onehot, taper.astype(jnp.float32)).astype(jnp.bfloat16)


def body(
    field,
    ens,
    sdev,
    lon_taper,
    static_taper,
    loc_vert,
    static_vert,
    obs_block,
    obs_value,
    obs_rinv,
    obs_horiz,
    obs_vert,
):
    members, lev_rows, lon_cols, lat_rows = ens.shape
    half = lon_taper.shape[0] // 2
    zpert = (ens.astype(jnp.float32) * field[None]).astype(jnp.bfloat16)
    spart = (sdev * field).astype(jnp.bfloat16)[None]
    zwide, swide = (padded(zpert, (("lon", 2),), half), padded(spart, (("lon", 2),), half))
    zsmooth = jnp.einsum(
        "klea,ei->klia", zwide, band_matrix(lon_taper, lon_cols), preferred_element_type=jnp.float32
    ).astype(jnp.bfloat16)
    ssmooth = jnp.einsum(
        "klea,ei->klia",
        swide,
        band_matrix(static_taper, lon_cols),
        preferred_element_type=jnp.float32,
    ).astype(jnp.bfloat16)
    full_loc, full_static = side_by_side((loc_vert, static_vert), "lev", 0, 1)
    zcols, scols, ecols = sent_together((zsmooth, ssmooth, ens), "lev", 2, 1, 0)
    zvert = jnp.einsum("lm,kmia->klia", full_loc, zcols, preferred_element_type=jnp.float32)
    ens_cols = jnp.sum(ecols.astype(jnp.float32) * zvert, axis=0)[None]
    static_cols = jnp.einsum(
        "lm,kmia->klia", full_static, scols, preferred_element_type=jnp.float32
    )
    ens_back, static_back = sent_together((ens_cols, static_cols), "lev", 1, 2, 0)
    ens_sum = ens_back[0]
    static_sum = static_back[0]
    increment = ens_weight * ens_sum + static_weight * sdev * static_sum
    block_lon = lon_cols // 8
    block_lat = lat_rows // 16
    nblk = block_lon * block_lat
    slots = obs_block.shape[0]
    blocks = (
        increment.reshape(lev_rows, block_lon, 8, block_lat, 16)
        .transpose(0, 1, 3, 2, 4)
        .reshape(lev_rows * nblk, 128)
    )
    live = obs_block >= 0
    local_ids = obs_block - lax.axis_index("lon") * nblk
    safe = jnp.where(live, local_ids, 0)
    selector = ((jnp.arange(nblk)[:, None] == safe[None, :]) & live[None, :]).astype(jnp.float32)
    vert_rows = obs_vert.T
    projected = jnp.dot(blocks, obs_horiz.T, precision=lax.Precision.HIGHEST).reshape(
        lev_rows, nblk, slots
    )
    picked = jnp.sum(projected * selector[None], axis=1)
    partial_value = jnp.sum(picked * vert_rows, axis=0)
    hx = taken_together(partial_value, "lev")
    miss = hx - obs_value
    dep = jnp.where(live, obs_rinv * miss, 0.0)
    obs_cost = taken_together(0.5 * jnp.sum(dep * miss), "lon")
    weights = vert_rows * dep[None, :]
    spread = (weights[:, None, :] * selector[None]).reshape(lev_rows * nblk, slots)
    adj_blocks = jnp.dot(spread, obs_horiz, precision=lax.Precision.HIGHEST)
    adjoint_field = (
        adj_blocks.reshape(lev_rows, block_lon, block_lat, 8, 16)
        .transpose(0, 1, 3, 2, 4)
        .reshape(lev_rows, lon_cols, lat_rows)
    )
    return (increment, adjoint_field, obs_cost)


def solution(mesh):
    return jax.shard_map(
        body,
        mesh=mesh,
        in_specs=(
            P("lev", "lon", None),
            P(None, "lev", "lon", None),
            P("lev", "lon", None),
            P(),
            P(),
            P("lev", None),
            P("lev", None),
            P("lon"),
            P("lon"),
            P("lon"),
            P("lon", None),
            P("lon", "lev"),
        ),
        out_specs=(P("lev", "lon", None), P("lev", "lon", None), P()),
        check_vma=False,
    )
```

profile of v0, /device:TPU:1, one launch (start us, length us, event | category | flops | bytes accessed | tf_op | source)
XLA Modules:
  0.0 373.3 jit_solution(6776272283396366946)
XLA Ops:
  0.6 3.8 %multiply_convert_fusion = bf16[80,18,16,128]{3,2,1,0:T(8,128)(2,1)S(1)} fusion(bf16[80,18,16,128]{3,2,1,0:T(8,128)(2,1)} %param.13, f32[18,16,128]{2,1,0:T(8,128)} %param.12), kind=kLoop, calls=%fused_computation.10 | loop fusion | flops 8847360 | bytes 11943936 | tf_op jit(solution)/shard_map/convert_element_type | solution.py:79
  4.5 3.1 fusion.42
  7.9 9.1 %collective-permute-start.1 = (bf16[80,18,8,128]{3,2,1,0:T(8,128)(2,1)}, bf16[80,18,8,128]{3,2,1,0:T(8,128)(2,1)}, u32[]{:S(2)}, u32[]{:S(2)}) collective-permute-start(bf16[80,18,8,128]{3,2,1,0:T(8,128)(2,1)} %get-tuple-element.10), channel_id=1, source_target_pairs={{4,0},{8,4},{12,8},{16,12},{20,16},{24,20},{28,24},{32,28},{36,32}... | collective-permute-start | bytes 8847368 | tf_op jit(solution)/shard_map/ppermute | solution.py:19
  17.0 7.2 %collective-permute-start.3 = (bf16[1,18,8,128]{3,2,1,0:T(8,128)(2,1)S(1)}, bf16[1,18,8,128]{3,2,1,0:T(8,128)(2,1)S(1)}, u32[]{:S(2)}, u32[]{:S(2)}) collective-permute-start(bf16[1,18,8,128]{3,2,1,0:T(8,128)(2,1)S(1)} %get-tuple-element.14), channel_id=1, source_target_pairs={{4,0},{8,4},{12,8},{16,12},{20,16},{24,20},{28,24},{32,28},{36,32}... | collective-permute-start | bytes 110600 | tf_op jit(solution)/shard_map/ppermute | solution.py:19
  25.4 115.6 %collective-permute-done.3 = bf16[1,18,8,128]{3,2,1,0:T(8,128)(2,1)S(1)} collective-permute-done((bf16[1,18,8,128]{3,2,1,0:T(8,128)(2,1)S(1)}, bf16[1,18,8,128]{3,2,1,0:T(8,128)(2,1)S(1)}, u32[]{:S(2)}, u32[]{:S(2)}) %collective-permute-start.3) | collective-permute-done | bytes 36896 | tf_op jit(solution)/shard_map/ppermute | solution.py:19
  141.0 0.8 collective-permute-done.2
  142.0 5.6 %convert_bitcast_fusion = bf16[80,18,16,128]{3,2,1,0:T(8,128)(2,1)S(1)} fusion(bf16[80,18,8,128]{3,2,1,0:T(8,128)(2,1)} %collective-permute-done.1, bf16[80,18,16,128]{3,2,1,0:T(8,128)(2,1)} %copy-done.2, bf16[80,18,8,128]{3,2,1,0:T(8,128)(2,1)} %collective-permute-done, bf16[1,32,16]{1,2,0:T(8,128)(2,1)S(1)} %copy.120), kind=kOutput, calls=%fused_computation.14 | convolution fusion | flops 227082240 | bytes 17695744 | tf_op jit(solution)/shard_map/klea,ei->klia/dot_general | solution.py:82
  148.0 1.2 pad_maximum_fusion
  149.2 13.7 %copy.106 = bf16[161,18,16,128]{3,0,1,2:T(8,128)(2,1)} copy(bf16[161,18,16,128]{3,2,1,0:T(8,128)(2,1)S(1)} %pad_maximum_fusion) | data formatting | bytes 23740416 | tf_op jit(solution)/shard_map/concatenate | solution.py:34
  162.9 6.9 %all-to-all-start = ((bf16[161,18,16,128]{3,0,1,2:T(8,128)(2,1)}), bf16[161,18,16,128]{3,0,1,2:T(8,128)(2,1)}, u32[]{:S(2)}, u32[]{:S(2)}) async-start(bf16[161,18,16,128]{3,0,1,2:T(8,128)(2,1)} %copy.106), calls=%async_computation | async-start | bytes 24772608 | tf_op jit(solution)/shard_map/all_to_all | solution.py:36
  169.8 136.8 %all-gather = bf16[4,18,144]{2,1,0:T(8,128)(2,1)S(1)} all-gather(bf16[1,18,144]{2,1,0:T(8,128)(2,1)S(1)} %maximum_bitcast_fusion.2), channel_id=1, replica_groups=mesh['lon'=32,'lev'=4] {'lev'}, dimensions={0}, use_global_device_ids=true | all-gather | bytes 25920 | tf_op jit(solution)/shard_map/all_gather | solution.py:26
  306.7 6.1 %copy.139 = bf16[161,18,4,4,128]{4,0,3,1,2:T(8,128)(2,1)S(1)} copy(bf16[161,18,4,4,128]{4,0,1,3,2:T(8,128)(2,1)} %bitcast.12) | data formatting | bytes 23740416 | tf_op jit(solution)/shard_map/all_to_all | solution.py:36
  312.9 4.5 %fusion.41 = (bf16[80,4,18,4,128]{4,0,3,2,1:T(8,128)(2,1)S(1)}, bf16[80,4,18,4,128]{4,0,3,2,1:T(8,128)(2,1)}) fusion(bf16[161,4,18,4,128]{4,0,3,2,1:T(8,128)(2,1)S(1)} %bitcast.98), kind=kLoop, calls=%fused_computation.66 | loop fusion | bytes 23592960 | tf_op jit(solution)/shard_map/slice | solution.py:41
  317.5 4.3 %bitcast_convert_fusion = f32[80,72,4,128]{3,0,2,1:T(8,128)S(1)} fusion(bf16[80,4,18,4,128]{4,0,3,2,1:T(8,128)(2,1)} %get-tuple-element.8), kind=kLoop, calls=%fused_computation.11 | loop fusion | flops 2949120 | bytes 17694720 | tf_op jit(solution)/shard_map/convert_element_type | solution.py:94
  322.1 10.5 %fusion.6 = f32[72,4,128]{2,0,1:T(8,128)S(1)} fusion(f32[80,72,4,128]{3,0,2,1:T(8,128)S(1)} %bitcast_convert_fusion, bf16[80,72,4,128]{3,0,2,1:T(8,128)(2,1)S(1)} %bitcast.101, bf16[72,144]{1,0:T(8,128)(2,1)S(1)} %reshape.131), kind=kOutput, calls=%fused_computation.9 | convolution fusion | flops 430534656 | bytes 17860608 | tf_op jit(solution)/shard_map/lm,kmia->klia/dot_general | solution.py:93
  333.4 3.6 all-to-all-start.1
  337.0 5.4 %all-to-all-done.1 = f32[2,72,4,128]{3,2,0,1:T(4,128)S(1)} async-done(((f32[2,72,4,128]{3,2,0,1:T(4,128)}), f32[2,72,4,128]{3,2,0,1:T(4,128)S(1)}, u32[]{:S(2)}, u32[]{:S(2)}) %all-to-all-start.1) | async-done | bytes 294944 | tf_op jit(solution)/shard_map/all_to_all | solution.py:36
  343.6 1.2 fusion.13
  345.4 4.2 %all-to-all-start.2 = ((f32[4,1,1024]{2,1,0:T(1,128)}), f32[4,1,1024]{2,1,0:T(1,128)S(1)}, u32[]{:S(2)}, u32[]{:S(2)}) async-start(f32[4,1,1024]{2,1,0:T(1,128)} %broadcast_in_dim.15), calls=%async_computation.2 | async-start | bytes 32768 | tf_op jit(solution)/shard_map/all_to_all | solution.py:48
  349.9 2.8 all-to-all-done.2
  354.7 9.6 %all-to-all-start.3 = ((f32[32,1,1]{2,1,0:T(1,128)}), f32[32,1,1]{2,1,0:T(1,128)S(1)}, u32[]{:S(2)}, u32[]{:S(2)}) async-start(f32[32,1,1]{2,1,0:T(1,128)} %broadcast_in_dim.17), calls=%async_computation.3 | async-start | bytes 32768 | tf_op jit(solution)/shard_map/all_to_all | solution.py:48
  364.3 3.9 %convolution_bitcast_fusion = f32[18,2,8,8,16]{4,3,2,1,0:T(8,128)S(1)} fusion(f32[8,16,1024,1,1]{2,1,0,4,3:T(8,128)S(1)} %bitcast.107, f32[2,8,1024]{2,1,0:T(8,128)S(1)} %and_convert_fusion, f32[18,1024]{1,0:T(8,128)S(1)} %bitcast_multiply_fusion.1), kind=kOutput, calls=%fused_computation.15 | convolution fusion | flops 453279744 | bytes 811008 | tf_op jit(solution)/shard_map/dot_general | solution.py:127
  368.1 1.0 reshape.128
  369.1 3.5 all-to-all-done.3
  (73 shorter events, 7.3 us)
Async XLA Ops:
  0.6 23.6 %copy-start = (bf16[17]{0:T(256)(128)(2,1)S(1)}, bf16[17]{0:T(256)(128)(2,1)}, u32[]{:S(2)}) copy-start(bf16[17]{0:T(256)(128)(2,1)} %param.16) | copy-start | bytes 106
  4.5 3.4 copy-start.2
  4.5 12.5 %copy-start.4 = (f32[18,16,128]{2,1,0:T(8,128)S(1)}, f32[18,16,128]{2,1,0:T(8,128)}, u32[]{:S(2)}) copy-start(f32[18,16,128]{2,1,0:T(8,128)} %param.14) | copy-start | bytes 442372
  4.5 12.5 %copy-start.6 = (f32[18,16,128]{2,1,0:T(8,128)S(1)}, f32[18,16,128]{2,1,0:T(8,128)}, u32[]{:S(2)}) copy-start(f32[18,16,128]{2,1,0:T(8,128)} %param.12) | copy-start | bytes 442372
  4.5 20.2 %copy-start.13 = (bf16[17]{0:T(256)(128)(2,1)S(1)}, bf16[17]{0:T(256)(128)(2,1)}, u32[]{:S(2)}) copy-start(bf16[17]{0:T(256)(128)(2,1)} %param.15) | copy-start | bytes 106
  7.9 134.1 %collective-permute-start.1 = (bf16[80,18,8,128]{3,2,1,0:T(8,128)(2,1)}, bf16[80,18,8,128]{3,2,1,0:T(8,128)(2,1)}, u32[]{:S(2)}, u32[]{:S(2)}) collective-permute-start(bf16[80,18,8,128]{3,2,1,0:T(8,128)(2,1)} %get-tuple-element.10), channel_id=1, source_target_pairs={{4,0},{8,4},{12,8},{16,12},{20,16},{24,20},{28,24},{32,28},{36,32}... | collective-permute-start | bytes 8847368 | tf_op jit(solution)/shard_map/ppermute | solution.py:19
  16.9 125.0 %collective-permute-start = (bf16[80,18,8,128]{3,2,1,0:T(8,128)(2,1)S(1)}, bf16[80,18,8,128]{3,2,1,0:T(8,128)(2,1)}, u32[]{:S(2)}, u32[]{:S(2)}) collective-permute-start(bf16[80,18,8,128]{3,2,1,0:T(8,128)(2,1)S(1)} %get-tuple-element.9), channel_id=1, source_target_pairs={{0,4},{4,8},{8,12},{12,16},{16,20},{20,24},{24,28},{28,32},{32,36}... | collective-permute-start | bytes 8847368 | tf_op jit(solution)/shard_map/ppermute | solution.py:16
  17.0 124.0 %collective-permute-start.3 = (bf16[1,18,8,128]{3,2,1,0:T(8,128)(2,1)S(1)}, bf16[1,18,8,128]{3,2,1,0:T(8,128)(2,1)S(1)}, u32[]{:S(2)}, u32[]{:S(2)}) collective-permute-start(bf16[1,18,8,128]{3,2,1,0:T(8,128)(2,1)S(1)} %get-tuple-element.14), channel_id=1, source_target_pairs={{4,0},{8,4},{12,8},{16,12},{20,16},{24,20},{28,24},{32,28},{36,32}... | collective-permute-start | bytes 110600 | tf_op jit(solution)/shard_map/ppermute | solution.py:19
  24.2 117.5 %collective-permute-start.2 = (bf16[1,18,8,128]{3,2,1,0:T(8,128)(2,1)S(1)}, bf16[1,18,8,128]{3,2,1,0:T(8,128)(2,1)S(1)}, u32[]{:S(2)}, u32[]{:S(2)}) collective-permute-start(bf16[1,18,8,128]{3,2,1,0:T(8,128)(2,1)S(1)} %get-tuple-element.13), channel_id=1, source_target_pairs={{0,4},{4,8},{8,12},{12,16},{16,20},{20,24},{24,28},{28,32},{32,36}... | collective-permute-start | bytes 110600 | tf_op jit(solution)/shard_map/ppermute | solution.py:16
  141.8 5.8 %slice-start = ((s8[5898240]{0:T(1024)(128)(4,1)}), s8[4194304]{0:T(1024)(128)(4,1)S(1)}, s32[]{:S(2)}) async-start(s8[5898240]{0:T(1024)(128)(4,1)} %bitcast.99), calls=%async_computation.4 | async-start | bytes 8388608
  141.9 6.0 %slice-start.1 = ((s8[5898240]{0:T(1024)(128)(4,1)}), s8[1703936]{0:T(1024)(128)(4,1)S(1)}, s32[]{:S(2)}) async-start(s8[5898240]{0:T(1024)(128)(4,1)} %bitcast.99), calls=%async_computation.5 | async-start | bytes 3407872
  162.9 6.9 %copy-start.8 = (bf16[18,72]{1,0:T(8,128)(2,1)S(1)}, bf16[18,72]{1,0:T(8,128)(2,1)}, u32[]{:S(2)}) copy-start(bf16[18,72]{1,0:T(8,128)(2,1)} %param.18) | copy-start | bytes 7780
  162.9 6.9 %copy-start.9 = (bf16[18,72]{1,0:T(8,128)(2,1)S(1)}, bf16[18,72]{1,0:T(8,128)(2,1)}, u32[]{:S(2)}) copy-start(bf16[18,72]{1,0:T(8,128)(2,1)} %param.17) | copy-start | bytes 7780
  162.9 143.8 %copy-start.10 = (s32[1024]{0:T(1024)S(1)}, s32[1024]{0:T(1024)}, u32[]{:S(2)}) copy-start(s32[1024]{0:T(1024)} %param.19) | copy-start | bytes 12292
  162.9 143.8 %all-to-all-start = ((bf16[161,18,16,128]{3,0,1,2:T(8,128)(2,1)}), bf16[161,18,16,128]{3,0,1,2:T(8,128)(2,1)}, u32[]{:S(2)}, u32[]{:S(2)}) async-start(bf16[161,18,16,128]{3,0,1,2:T(8,128)(2,1)} %copy.106), calls=%async_computation | async-start | bytes 24772608 | tf_op jit(solution)/shard_map/all_to_all | solution.py:36
  332.5 11.0 %copy-start.3 = (f32[1024,128]{1,0:T(8,128)S(1)}, f32[1024,128]{1,0:T(8,128)}, u32[]{:S(2)}) copy-start(f32[1024,128]{1,0:T(8,128)} %param.22) | copy-start | bytes 1572868
  332.6 12.2 %copy-start.7 = (f32[1024,18]{0,1:T(8,128)S(1)}, f32[1024,18]{0,1:T(8,128)}, u32[]{:S(2)}) copy-start(f32[1024,18]{0,1:T(8,128)} %param.23) | copy-start | bytes 221188
  332.6 20.2 %copy-start.11 = (f32[1024]{0:T(1024)S(1)}, f32[1024]{0:T(1024)}, u32[]{:S(2)}) copy-start(f32[1024]{0:T(1024)} %param.21) | copy-start | bytes 12292
  332.6 20.2 %copy-start.12 = (f32[1024]{0:T(1024)S(1)}, f32[1024]{0:T(1024)}, u32[]{:S(2)}) copy-start(f32[1024]{0:T(1024)} %param.20) | copy-start | bytes 12292
  333.4 9.0 %all-to-all-start.1 = ((f32[2,72,4,128]{3,2,0,1:T(4,128)}), f32[2,72,4,128]{3,2,0,1:T(4,128)S(1)}, u32[]{:S(2)}, u32[]{:S(2)}) async-start(f32[2,72,4,128]{3,2,0,1:T(4,128)} %copy.112), calls=%async_computation.1 | async-start | bytes 589824 | tf_op jit(solution)/shard_map/all_to_all | solution.py:36
  342.6 26.5 %copy-start.5 = (f32[18,16,128]{2,1,0:T(8,128)}, f32[18,16,128]{2,1,0:T(8,128)S(1)}, u32[]{:S(2)}) copy-start(f32[18,16,128]{2,1,0:T(8,128)S(1)} %multiply_add_fusion) | copy-start | bytes 442372
  342.6 30.7 %copy-start.1 = (bf16[17]{0:T(256)(128)(2,1)S(1)}, bf16[17]{0:T(256)(128)(2,1)}, u32[]{:S(2)}) copy-start(bf16[17]{0:T(256)(128)(2,1)} %param.16) | copy-start | bytes 106
  345.4 7.3 %all-to-all-start.2 = ((f32[4,1,1024]{2,1,0:T(1,128)}), f32[4,1,1024]{2,1,0:T(1,128)S(1)}, u32[]{:S(2)}, u32[]{:S(2)}) async-start(f32[4,1,1024]{2,1,0:T(1,128)} %broadcast_in_dim.15), calls=%async_computation.2 | async-start | bytes 32768 | tf_op jit(solution)/shard_map/all_to_all | solution.py:48
  354.7 18.0 %all-to-all-start.3 = ((f32[32,1,1]{2,1,0:T(1,128)}), f32[32,1,1]{2,1,0:T(1,128)S(1)}, u32[]{:S(2)}, u32[]{:S(2)}) async-start(f32[32,1,1]{2,1,0:T(1,128)} %broadcast_in_dim.17), calls=%async_computation.3 | async-start | bytes 32768 | tf_op jit(solution)/shard_map/all_to_all | solution.py:48
where the time goes:
time: 374 us; the launch traced here: 373 us
  blocking collectives  137 us (37%)
  waiting for transfers between devices  128 us (34%)
  starting transfers between devices  40.5 us (11%)
  local copies, waits for them, and re-layouts  32.7 us (9%)
  matrix products  22.4 us (6%)
  other arithmetic  11 us (3%)
    all_gather x1, blocking collectives, side_by_side(): whole, at, done = (lax.all_gather(both, axis, axis=dim, tiled=True), 0, [])  137 us
    ppermute x2, waiting for transfers between devices, padded(): lax.ppermute(lax.slice_in_dim(block, 0, width, axis=dim), axis, backward)  116 us
    ppermute x2, starting transfers between devices, padded(): lax.ppermute(lax.slice_in_dim(block, 0, width, axis=dim), axis, backward)  16.3 us
    concatenate x2, local copies, waits for them, and re-layouts, sent_together(): both = jnp.concatenate(arrays, axis=along)  14.4 us
    all_to_all x2, starting transfers between devices, sent_to_all(): return lax.all_to_all(copies, axis, split_axis=0, concat_axis=0, tiled=True)  13.8 us
    dot_general x1, matrix products, body(): jnp.einsum('lm,kmia->klia', full_loc, zcols, preferred_element_type=jnp.f...  10.5 us
    all_to_all x2, starting transfers between devices, sent_together(): lax.all_to_all(both, axis, split_axis=split_dim, concat_axis=concat_dim,...  10.4 us
  transfers between devices with their start and end apart: 8, of which 5 were waited for; matrix products, arithmetic and copies ran while one was open for 2% of the time, Pallas kernels for 0%

commit v1 on v0

v1 whole, which is shorter than its diff:
```python
import functools

import jax
import jax.numpy as jnp
from jax import lax
from jax.experimental import pallas as pl
from jax.experimental.pallas import tpu as pltpu
from jax.sharding import PartitionSpec as P

MESH = pl.DeviceIdType.MESH
F32 = jnp.float32
BF16 = jnp.bfloat16

ens_weight = 0.8
static_weight = 0.5

COLUMNS = 16
PEERS = 8
CHUNKS = 5
PAIR = 2
OWN = CHUNKS * PAIR
LEVELS = 72
ROWS = 18
QUADS = LEVELS // 4


def iota(shape, dim):
    return lax.broadcasted_iota(jnp.int32, shape, dim)


def band(taper, out):
    row, col = iota((128, 192), 0), iota((128, 192), 1)
    at = col % 48 - (row // 32) * 8 - row % 8
    same = (row // 8) % 4 == col // 48
    total = jnp.zeros((128, 192), F32)
    for d in range(17):
        total = total + jnp.where(at == d, taper[:, d : d + 1].astype(F32), 0.0)
    out[...] = jnp.where(same, total, 0.0).astype(BF16)


def spread(matrix):
    cols = (iota((LEVELS, 576), 0) == iota((LEVELS, 576), 1) // 8).astype(BF16)
    rows = (iota((144, ROWS), 0) // 8 == iota((144, ROWS), 1)).astype(BF16)
    wide = jnp.dot(matrix.astype(BF16), cols, preferred_element_type=F32).astype(BF16)
    tall = jnp.dot(rows, wide, preferred_element_type=F32)
    keep = iota((144, 576), 0) % 8 == iota((144, 576), 1) % 8
    return jnp.where(keep, tall, 0.0).astype(BF16)


def kernel(
    ens, field, spart, sdev, loc, loc_v, svert, ltaper, staper, out,
    ens_buf, field_buf, spart_buf, loc_buf, zh_buf, band_e, band_s, vert_e, vert_s, acc, sv_buf, ret_buf,
    es_send, es_recv, ey_send, ey_recv, f_send, f_recv, fy_send, fy_recv, l_send, l_recv, r_send, r_recv,
):
    lon, q = lax.axis_index("lon"), lax.axis_index("lev")
    column, h = lon // 2, lon % 2
    zlo, core = q // 2, q % 2
    left = 2 * ((column + COLUMNS - 1) % COLUMNS) + h
    right = 2 * ((column + 1) % COLUMNS) + h

    def peer(r):
        hr = 1 - h if r & 4 else h
        zr = 1 - zlo if r & 2 else zlo
        cr = 1 - core if r & 1 else core
        return hr, 2 * zr + cr

    barrier = pltpu.get_barrier_semaphore()
    for r in range(1, PEERS):
        hr, qr = peer(r)
        pl.semaphore_signal(barrier, inc=1, device_id=(2 * column + hr, qr), device_id_type=MESH)
    for side in (left, right):
        pl.semaphore_signal(barrier, inc=1, device_id=(side, q), device_id_type=MESH)
    pl.semaphore_wait(barrier, PEERS + 1)

    def remote(src, dst, send, recv, where):
        return pltpu.make_async_remote_copy(
            src_ref=src, dst_ref=dst, send_sem=send, recv_sem=recv, device_id=where, device_id_type=MESH
        )

    def column_device(r):
        hr, qr = peer(r)
        return (2 * column + hr, qr)

    pairs = ((field, field_buf), (spart, spart_buf))

    def f_slot(n, r):
        hr, qr = peer(r)
        return pairs[n][1].at[pl.ds(ROWS * qr, ROWS), pl.ds(1 + 2 * hr, 2)]

    def f_copy(n, r):
        if r == 0:
            return pltpu.make_async_copy(pairs[n][0], f_slot(n, 0), f_recv.at[n, 0])
        return remote(pairs[n][0], f_slot(n, 0), f_send.at[n, r], f_recv.at[n, r], column_device(r))

    def f_pass(n, r):
        return remote(f_slot(n, r), f_slot(n, r), f_send.at[n, r + 1], f_recv.at[n, r + 1], column_device(1))

    def f_arrived(n, r):
        if r == 0:
            return f_copy(n, 0).wait()
        remote(f_slot(n, r), f_slot(n, r), f_send.at[n, r], f_recv.at[n, r], column_device(r)).wait_recv()

    def l_copy(r):
        return remote(loc, loc_buf.at[q], l_send.at[r], l_recv.at[r], column_device(r))

    def l_arrived(r):
        hr, qr = peer(r)
        remote(loc, loc_buf.at[qr], l_send.at[r], l_recv.at[r], column_device(r)).wait_recv()

    def e_copy(c, half, r):
        hr, qr = peer(r)
        here = h if half == 0 else 1 - h
        there = 1 + 3 * h if half == 0 else 2 + h
        src = ens.at[pl.ds(OWN * (4 * hr + qr) + PAIR * c, PAIR), :, here]
        dst = ens_buf.at[c, :, pl.ds(ROWS * q, ROWS), there]
        if r == 0:
            return pltpu.make_async_copy(src, dst, es_recv.at[c, half, 0])
        return remote(src, dst, es_send.at[c, half, r], es_recv.at[c, half, r], column_device(r))

    def e_arrived(c, half):
        e_copy(c, half, 0).wait()
        for r in range(1, PEERS):
            hr, qr = peer(r)
            there = 1 + 3 * hr if half == 0 else 2 + hr
            slot = ens_buf.at[c, :, pl.ds(ROWS * qr, ROWS), there]
            remote(slot, slot, es_send.at[c, half, r], es_recv.at[c, half, r], column_device(r)).wait_recv()

    def sides(buf, send, recv, lead):
        mine = [buf.at[lead + (slice(None), 1)], buf.at[lead + (slice(None), 4)]]
        theirs = [buf.at[lead + (slice(None), 5)], buf.at[lead + (slice(None), 0)]]
        return [
            remote(mine[s], theirs[s], send.at[s], recv.at[s], ((left, right)[s], q)) for s in range(2)
        ]

    def e_sides(c):
        return [s for k in range(PAIR) for s in sides(ens_buf, ey_send.at[c, k], ey_recv.at[c, k], (c, k))]

    def f_sides():
        return sides(field_buf, fy_send.at[0], fy_recv.at[0], ()) + sides(
            spart_buf, fy_send.at[1], fy_recv.at[1], ()
        )

    order = (4, 6, 7, 5, 2, 3, 1)
    for n in range(2):
        for r in (4, 6, 2, 1, 0):
            f_copy(n, r).start()
    for r in (2, 3, 1):
        l_copy(r).start()

    def send_members(c, half):
        for r in order:
            e_copy(c, half, r).start()
        e_copy(c, half, 0).start()

    send_members(0, 0)
    for c in range(1, CHUNKS):
        send_members(c, 0)
        send_members(c - 1, 1)
    send_members(CHUNKS - 1, 1)

    band(ltaper[...], band_e)
    band(staper[...], band_s)
    vert_s[...] = spread(svert[...])
    vert_e[pl.ds(144 * q, 144)] = spread(loc_v[...])
    for r in (1, 2, 3):
        l_arrived(r)
        hr, qr = peer(r)
        vert_e[pl.ds(144 * qr, 144)] = spread(loc_buf[qr])
    acc[...] = jnp.zeros_like(acc)

    for r in (2, 6, 4):
        for n in range(2):
            f_arrived(n, r)
            f_pass(n, r).start()
    for n in range(2):
        for r in (0, 1, 3, 5, 7):
            f_arrived(n, r)
    for s in f_sides():
        s.start()

    def smooth(weights, read):
        def quad(n, _):
            out_rows = jnp.dot(weights[...], read(4 * n), preferred_element_type=F32).astype(BF16)
            lanes = out_rows.shape[1]
            for ib in range(4):
                zh_buf[ib, pl.ds(pl.multiple_of(32 * n, 32), 32), :lanes] = out_rows[32 * ib : 32 * ib + 32]
            return 0

        lax.fori_loop(0, QUADS, quad, 0)

    def read_static(m):
        return spart_buf[pl.ds(m, 4)].astype(F32).reshape(192, 128).astype(BF16)

    def members(c):
        def read(m):
            weight = field_buf[pl.ds(m, 4)]
            both = [(ens_buf[c, k, pl.ds(m, 4)].astype(F32) * weight).reshape(192, 128) for k in range(PAIR)]
            return jnp.concatenate(both, axis=1).astype(BF16)

        smooth(band_e, read)

        def part(n, _):
            ib, third = n // 3, n % 3
            rows = pl.ds(pl.multiple_of(192 * third, 192), 192)
            levels = pl.ds(24 * third, 24)
            mixed = jnp.dot(vert_e[rows], zh_buf[ib], preferred_element_type=F32)
            total = acc[ib, levels]
            for k in range(PAIR):
                value = mixed[:, 128 * k : 128 * k + 128].reshape(24, 8, 128)
                total = total + ens_buf[c, k, levels, 1 + ib].astype(F32) * value
            acc[ib, levels] = total
            return 0

        lax.fori_loop(0, 12, part, 0)

    e_arrived(0, 0)
    for s in e_sides(0):
        s.start()
    for s in f_sides():
        s.wait()
    smooth(band_s, read_static)
    for i in range(2):
        sv = jnp.dot(vert_s[...], zh_buf[2 * h + i, :, :128], preferred_element_type=F32)
        sv_buf[i] = sv.reshape(ROWS, 8, 128)

    def chunk(c, _):
        @pl.when(c + 1 < CHUNKS)
        def _():
            e_arrived(c + 1, 0)
            for s in e_sides(c + 1):
                s.start()

        e_arrived(c, 1)
        for s in e_sides(c):
            s.wait()
        members(c)
        return 0

    lax.fori_loop(0, CHUNKS, chunk, 0)

    def r_copy(r):
        hr, qr = peer(r)
        return remote(
            acc.at[pl.ds(2 * hr, 2), pl.ds(ROWS * qr, ROWS)], ret_buf.at[r], r_send.at[r], r_recv.at[r], column_device(r)
        )

    for r in order:
        r_copy(r).start()
    for r in order:
        r_copy(r).wait_recv()
    for i in range(2):
        total = acc[2 * h + i, pl.ds(ROWS * q, ROWS)]
        for r in range(1, PEERS):
            total = total + ret_buf[r, i]
        out[:, i] = ens_weight * total + static_weight * sdev[:, i] * sv_buf[i]

    for r in range(1, PEERS):
        r_copy(r).wait_send()
    for r in (1, 2, 3):
        l_copy(r).wait_send()
    for n in range(2):
        for r in (1, 2, 4, 6):
            f_copy(n, r).wait_send()
        for r in (2, 4, 6):
            f_pass(n, r).wait_send()

    def sent(c, _):
        for half in range(2):
            for r in range(1, PEERS):
                e_copy(c, half, r).wait_send()
        return 0

    lax.fori_loop(0, CHUNKS, sent, 0)


def increment_of(field, ens, sdev, lon_taper, static_taper, loc_vert, static_vert):
    members = ens.shape[0]
    spart = (sdev * field).astype(BF16).reshape(ROWS, 2, 8, 128)
    vmem = pl.BlockSpec(memory_space=pltpu.VMEM)
    hbm = pl.BlockSpec(memory_space=pltpu.HBM)
    loc = loc_vert.astype(F32)
    dma = pltpu.SemaphoreType.DMA
    out = pl.pallas_call(
        kernel,
        out_shape=jax.ShapeDtypeStruct((ROWS, 2, 8, 128), F32),
        in_specs=[hbm, hbm, hbm, vmem, hbm, vmem, vmem, vmem, vmem],
        out_specs=vmem,
        scratch_shapes=[
            pltpu.VMEM((CHUNKS, PAIR, LEVELS, 6, 8, 128), BF16),
            pltpu.VMEM((LEVELS, 6, 8, 128), F32),
            pltpu.VMEM((LEVELS, 6, 8, 128), BF16),
            pltpu.VMEM((4, ROWS, LEVELS), F32),
            pltpu.VMEM((4, 576, 256), BF16),
            pltpu.VMEM((128, 192), BF16),
            pltpu.VMEM((128, 192), BF16),
            pltpu.VMEM((576, 576), BF16),
            pltpu.VMEM((144, 576), BF16),
            pltpu.VMEM((4, LEVELS, 8, 128), F32),
            pltpu.VMEM((2, ROWS, 8, 128), F32),
            pltpu.VMEM((PEERS, 2, ROWS, 8, 128), F32),
            dma((CHUNKS, 2, PEERS)),
            dma((CHUNKS, 2, PEERS)),
            dma((CHUNKS, PAIR, 2)),
            dma((CHUNKS, PAIR, 2)),
            dma((2, PEERS)),
            dma((2, PEERS)),
            dma((2, 2)),
            dma((2, 2)),
            dma((4,)),
            dma((4,)),
            dma((PEERS,)),
            dma((PEERS,)),
        ],
        compiler_params=pltpu.CompilerParams(
            collective_id=0, has_side_effects=True, vmem_limit_bytes=48 * 1024 * 1024
        ),
        name="members",
    )(
        ens.reshape(members, ROWS, 2, 8, 128),
        field.reshape(ROWS, 2, 8, 128),
        spart,
        sdev.reshape(ROWS, 2, 8, 128),
        loc,
        loc,
        static_vert,
        lon_taper[None],
        static_taper[None],
    )
    return out.reshape(ROWS, 16, 128)


def sent_to_all(x, axis):
    copies = jnp.broadcast_to(x, (lax.axis_size(axis), *x.shape))
    return lax.all_to_all(copies, axis, split_axis=0, concat_axis=0, tiled=True)


def taken_together(x, axis):
    return sent_to_all(x, axis).sum(axis=0)


def body(
    field,
    ens,
    sdev,
    lon_taper,
    static_taper,
    loc_vert,
    static_vert,
    obs_block,
    obs_value,
    obs_rinv,
    obs_horiz,
    obs_vert,
):
    _, lev_rows, lon_cols, lat_rows = ens.shape
    increment = increment_of(field, ens, sdev, lon_taper, static_taper, loc_vert, static_vert)
    block_lon = lon_cols // 8
    block_lat = lat_rows // 16
    nblk = block_lon * block_lat
    slots = obs_block.shape[0]
    blocks = (
        increment.reshape(lev_rows, block_lon, 8, block_lat, 16)
        .transpose(0, 1, 3, 2, 4)
        .reshape(lev_rows * nblk, 128)
    )
    live = obs_block >= 0
    local_ids = obs_block - lax.axis_index("lon") * nblk
    safe = jnp.where(live, local_ids, 0)
    selector = ((jnp.arange(nblk)[:, None] == safe[None, :]) & live[None, :]).astype(jnp.float32)
    vert_rows = obs_vert.T
    projected = jnp.dot(blocks, obs_horiz.T, precision=lax.Precision.HIGHEST).reshape(
        lev_rows, nblk, slots
    )
    picked = jnp.sum(projected * selector[None], axis=1)
    partial_value = jnp.sum(picked * vert_rows, axis=0)
    hx = taken_together(partial_value, "lev")
    miss = hx - obs_value
    dep = jnp.where(live, obs_rinv * miss, 0.0)
    obs_cost = taken_together(0.5 * jnp.sum(dep * miss), "lon")
    weights = vert_rows * dep[None, :]
    spread = (weights[:, None, :] * selector[None]).reshape(lev_rows * nblk, slots)
    adj_blocks = jnp.dot(spread, obs_horiz, precision=lax.Precision.HIGHEST)
    adjoint_field = (
        adj_blocks.reshape(lev_rows, block_lon, block_lat, 8, 16)
        .transpose(0, 1, 3, 2, 4)
        .reshape(lev_rows, lon_cols, lat_rows)
    )
    return (increment, adjoint_field, obs_cost)


def solution(mesh):
    return jax.shard_map(
        body,
        mesh=mesh,
        in_specs=(
            P("lev", "lon", None),
            P(None, "lev", "lon", None),
            P("lev", "lon", None),
            P(),
            P(),
            P("lev", None),
            P("lev", None),
            P("lon"),
            P("lon"),
            P("lon"),
            P("lon", None),
            P("lon", "lev"),
        ),
        out_specs=(P("lev", "lon", None), P("lev", "lon", None), P()),
        check_vma=False,
    )
```

time: 374 us -> 142 us (0.38)
  blocking collectives: 137 us -> 0 us
  waiting for transfers between devices: 128 us -> 6.53 us
  Pallas kernels: 0 us -> 106 us
  starting transfers between devices: 40.5 us -> 10.6 us
  local copies, waits for them, and re-layouts: 32.7 us -> 8.46 us
  matrix products: 22.4 us -> 5.02 us
  other arithmetic: 11 us -> 3.1 us
    all_gather x1 -> x0, blocking collectives: 137 us -> none  [side_by_side(): whole, at, done = (lax.all_gather(both, axis, axis=dim, tiled=True), 0, [])]
    ppermute x4 -> x0, waiting for transfers between devices: 116 us -> none  [the longest x2 116 us: padded(): lax.ppermute(lax.slice_in_dim(block, 0, width, axis=dim), axis, backward)]
    pallas_call x0 -> x1, Pallas kernels: none -> 106 us  [increment_of(): pl.pallas_call(kernel, out_shape=jax.ShapeDtypeStruct((ROWS, 2, 8, 128),...]
    dot_general x6 -> x0, matrix products: 17.4 us -> none  [the longest x1 10.5 us: body(): jnp.einsum('lm,kmia->klia', full_loc, zcols, preferred_element_type=jnp.f...]
    ppermute x4 -> x0, starting transfers between devices: 16.3 us -> none  [the longest x2 16.3 us: padded(): lax.ppermute(lax.slice_in_dim(block, 0, width, axis=dim), axis, backward)]
    concatenate x2 -> x0, local copies, waits for them, and re-layouts: 14.4 us -> none  [sent_together(): both = jnp.concatenate(arrays, axis=along)]
    all_to_all x2 -> x0, starting transfers between devices: 10.4 us -> none  [sent_together(): lax.all_to_all(both, axis, split_axis=split_dim, concat_axis=concat_dim,...]
    slice x5 -> x0, local copies, waits for them, and re-layouts: 7.72 us -> none  [the longest x3 4.65 us: sent_together(): done.append(lax.slice_in_dim(whole, at, at + a.shape[along], axis=along))]
  transfers between devices with their start and end apart: 8 -> 2, of which waited for: 5 -> 2; matrix products, arithmetic and copies ran while one was open for 2% -> 4% of each run, Pallas kernels for 0% -> 0%
where the time goes in v1:
time: 142 us; the launch traced here: 141 us
  Pallas kernels  106 us (75%)
  starting transfers between devices  10.6 us (7%)
  local copies, waits for them, and re-layouts  8.46 us (6%)
  waiting for transfers between devices  6.53 us (5%)
  matrix products  5.02 us (4%)
  other arithmetic  3.1 us (2%)
  between operations  1.46 us (1%)
    pallas_call x1, Pallas kernels, increment_of(): pl.pallas_call(kernel, out_shape=jax.ShapeDtypeStruct((ROWS, 2, 8, 128),...  106 us
    all_to_all x2, starting transfers between devices, sent_to_all(): return lax.all_to_all(copies, axis, split_axis=0, concat_axis=0, tiled=True)  10.6 us
    all_to_all x2, waiting for transfers between devices, sent_to_all(): return lax.all_to_all(copies, axis, split_axis=0, concat_axis=0, tiled=True)  6.53 us
    unnamed x22, local copies, waits for them, and re-layouts  5.33 us
    dot_general x1, matrix products, body(): adj_blocks = jnp.dot(spread, obs_horiz, precision=lax.Precision.HIGHEST)  3.84 us
  transfers between devices with their start and end apart: 2, of which 2 were waited for; matrix products, arithmetic and copies ran while one was open for 4% of the time, Pallas kernels for 0%

profile of v1, /device:TPU:1, one launch (start us, length us, event | category | flops | bytes accessed | tf_op | source)
XLA Modules:
  0.0 140.7 jit_solution(4906062849978853870)
XLA Ops:
  0.6 0.7 convert_element_type.17.loc.loc_v
  1.3 1.0 fusion.7.spart
  2.3 0.9 copy-done
  3.2 0.9 copy-done.1
  4.2 0.7 copy-done.2
  4.8 0.7 copy-done.3
  5.5 0.7 copy-done.4
  6.2 105.6 %members.1 = f32[18,2,8,128]{3,2,1,0:T(8,128)S(1)} custom-call(bf16[80,18,2,8,128]{4,3,2,1,0:T(8,128)(2,1)} %bitcast.44, f32[18,2,8,128]{3,2,1,0:T(8,128)S(1)} %bitcast.40, bf16[18,2,8,128]{3,2,1,0:T(8,128)(2,1)S(1)} %fusion.7.spart, f32[18,2,8,128]{3,2,1,0:T(8,128)S(1)} %bitcast.41, f32[18,72]{1,0:T(8,128)S(1)} %convert_element_type.17.loc.loc_v, ...), custom_call_target="tpu_custom_call" | custom-call | tf_op jit(solution)/shard_map/members/pallas_call | solution.py:283
  111.7 0.3 reshape_reshape.3
  112.4 0.3 dot_general.12
  112.7 0.3 copy-done.7
  113.1 0.3 copy-done.5
  113.4 1.2 fusion
  114.6 0.6 broadcast_in_dim.27
  115.2 4.6 %all-to-all-start = ((f32[4,1,1024]{2,1,0:T(1,128)}), f32[4,1,1024]{2,1,0:T(1,128)S(1)}, u32[]{:S(2)}, u32[]{:S(2)}) async-start(f32[4,1,1024]{2,1,0:T(1,128)} %broadcast_in_dim.27), calls=%async_computation | async-start | bytes 32768 | tf_op jit(solution)/shard_map/all_to_all | solution.py:334
  120.1 2.8 %all-to-all-done = f32[4,1,1024]{2,1,0:T(1,128)S(1)} async-done(((f32[4,1,1024]{2,1,0:T(1,128)}), f32[4,1,1024]{2,1,0:T(1,128)S(1)}, u32[]{:S(2)}, u32[]{:S(2)}) %all-to-all-start) | async-done | bytes 16416 | tf_op jit(solution)/shard_map/all_to_all | solution.py:334
  123.0 0.6 multiply_reduce_fusion
  124.3 0.6 broadcast_in_dim.29
  124.9 6.0 %all-to-all-start.1 = ((f32[32,1,1]{2,1,0:T(1,128)}), f32[32,1,1]{2,1,0:T(1,128)S(1)}, u32[]{:S(2)}, u32[]{:S(2)}) async-start(f32[32,1,1]{2,1,0:T(1,128)} %broadcast_in_dim.29), calls=%async_computation.1 | async-start | bytes 32768 | tf_op jit(solution)/shard_map/all_to_all | solution.py:334
  130.9 3.8 %convolution_bitcast_fusion = f32[18,2,8,8,16]{4,3,2,1,0:T(8,128)S(1)} fusion(f32[8,16,1024,1,1]{2,1,0,4,3:T(8,128)S(1)} %bitcast.46, f32[2,8,1024]{2,1,0:T(8,128)S(1)} %and_convert_fusion, f32[18,1024]{1,0:T(8,128)S(1)} %bitcast_multiply_fusion), kind=kOutput, calls=%fused_computation | convolution fusion | flops 453279744 | bytes 811008 | tf_op jit(solution)/shard_map/dot_general | solution.py:382
  134.8 1.0 reshape.108
  135.8 3.7 %all-to-all-done.1 = f32[32,1,1]{2,1,0:T(1,128)S(1)} async-done(((f32[32,1,1]{2,1,0:T(1,128)}), f32[32,1,1]{2,1,0:T(1,128)S(1)}, u32[]{:S(2)}, u32[]{:S(2)}) %all-to-all-start.1) | async-done | bytes 160 | tf_op jit(solution)/shard_map/all_to_all | solution.py:334
  139.4 0.6 reduce_sum.49
  140.1 0.7 copy.30
  (22 shorter events, 0.6 us)
Async XLA Ops:
  2.3 0.9 copy-start
  3.2 0.9 copy-start.1
  4.2 0.7 copy-start.2
  4.8 0.7 copy-start.3
  5.5 0.7 copy-start.4
  112.3 0.7 copy-start.7
  112.3 1.0 copy-start.5
  112.4 2.2 %copy-start.6 = (f32[1024,18]{0,1:T(8,128)S(1)}, f32[1024,18]{0,1:T(8,128)}, u32[]{:S(2)}) copy-start(f32[1024,18]{0,1:T(8,128)} %param.23) | copy-start | bytes 221188
  112.7 10.3 %copy-start.8 = (f32[1024]{0:T(1024)S(1)}, f32[1024]{0:T(1024)}, u32[]{:S(2)}) copy-start(f32[1024]{0:T(1024)} %param.21) | copy-start | bytes 12292
  112.7 10.3 %copy-start.9 = (f32[1024]{0:T(1024)S(1)}, f32[1024]{0:T(1024)}, u32[]{:S(2)}) copy-start(f32[1024]{0:T(1024)} %param.20) | copy-start | bytes 12292
  115.2 7.7 %all-to-all-start = ((f32[4,1,1024]{2,1,0:T(1,128)}), f32[4,1,1024]{2,1,0:T(1,128)S(1)}, u32[]{:S(2)}, u32[]{:S(2)}) async-start(f32[4,1,1024]{2,1,0:T(1,128)} %broadcast_in_dim.27), calls=%async_computation | async-start | bytes 32768 | tf_op jit(solution)/shard_map/all_to_all | solution.py:334
  124.9 14.6 %all-to-all-start.1 = ((f32[32,1,1]{2,1,0:T(1,128)}), f32[32,1,1]{2,1,0:T(1,128)S(1)}, u32[]{:S(2)}, u32[]{:S(2)}) async-start(f32[32,1,1]{2,1,0:T(1,128)} %broadcast_in_dim.29), calls=%async_computation.1 | async-start | bytes 32768 | tf_op jit(solution)/shard_map/all_to_all | solution.py:334

commit v2 on v1

v2 whole, which is shorter than its diff:
```python
import functools

import jax
import jax.numpy as jnp
from jax import lax
from jax.experimental import pallas as pl
from jax.experimental.pallas import tpu as pltpu
from jax.sharding import PartitionSpec as P

MESH = pl.DeviceIdType.MESH
F32 = jnp.float32
BF16 = jnp.bfloat16

ens_weight = 0.8
static_weight = 0.5

COLUMNS = 16
PEERS = 8
CHUNKS = 5
PAIR = 2
OWN = CHUNKS * PAIR
LEVELS = 72
ROWS = 18
QUADS = LEVELS // 4


def iota(shape, dim):
    return lax.broadcasted_iota(jnp.int32, shape, dim)


def band(taper, out):
    row, col = iota((128, 192), 0), iota((128, 192), 1)
    at = col % 48 - (row // 32) * 8 - row % 8
    same = (row // 8) % 4 == col // 48
    total = jnp.zeros((128, 192), F32)
    for d in range(17):
        total = total + jnp.where(at == d, taper[:, d : d + 1].astype(F32), 0.0)
    out[...] = jnp.where(same, total, 0.0).astype(BF16)


def spread(matrix):
    cols = (iota((LEVELS, 576), 0) == iota((LEVELS, 576), 1) // 8).astype(BF16)
    rows = (iota((144, ROWS), 0) // 8 == iota((144, ROWS), 1)).astype(BF16)
    wide = jnp.dot(matrix.astype(BF16), cols, preferred_element_type=F32).astype(BF16)
    tall = jnp.dot(rows, wide, preferred_element_type=F32)
    keep = iota((144, 576), 0) % 8 == iota((144, 576), 1) % 8
    return jnp.where(keep, tall, 0.0).astype(BF16)


def swapped(x):
    row, group = iota(x.shape, 1), iota(x.shape, 2) // 16
    for b in (1, 2, 4):
        row_bit, group_bit = (row // b) % 2, (group // b) % 2
        after = pltpu.roll(pltpu.roll(x, 8 - b, 1), 16 * b, 2)
        before = after if b == 4 else pltpu.roll(pltpu.roll(x, b, 1), 128 - 16 * b, 2)
        x = jnp.where(row_bit == group_bit, x, jnp.where(row_bit == 0, after, before))
    return x


def halves(x):
    high = x.astype(BF16)
    return high, (x - high.astype(F32)).astype(BF16)


def kernel(
    ens, field, sdev, ltaper, staper, loc, svert, block, value, rinv, horiz, vert,
    inc_out, adj_out, cost_out,
    ens_buf, field_buf, spart_buf, loc_buf, zh_buf, band_e, band_s, vert_e, vert_s, acc, sv_buf,
    d_buf, r_out, r_buf,
    field_v, sdev_v, svert_v, ltaper_v, staper_v, block_v, value_v, rinv_v, horiz_v, vert_v,
    pick, h_cat, h_turned, spread_hi, spread_lo, hx_all, cost_y, cost_x, cost_h,
    es_send, es_recv, ey_send, ey_recv, f_send, f_recv, fy_send, fy_recv, l_send, l_recv,
    d_send, d_recv, r_send, r_recv, x_send, x_recv, c_send, c_recv, in_sem,
):
    lon, q = lax.axis_index("lon"), lax.axis_index("lev")
    column, h = lon // 2, lon % 2
    zlo, core = q // 2, q % 2
    px, py = lon // 8, (lon // 2) % 4
    left = 2 * ((column + COLUMNS - 1) % COLUMNS) + h
    right = 2 * ((column + 1) % COLUMNS) + h

    def peer(r):
        hr = 1 - h if r & 4 else h
        zr = 1 - zlo if r & 2 else zlo
        cr = 1 - core if r & 1 else core
        return hr, 2 * zr + cr

    def column_device(r):
        hr, qr = peer(r)
        return (2 * column + hr, qr)

    def y_device(k):
        return (8 * px + 2 * ((py + k) % 4) + h, q)

    def x_device(k):
        return (8 * ((px + k) % 4) + 2 * py + h, q)

    early = [(field, field_v), (sdev, sdev_v), (loc, loc_buf.at[q]), (svert, svert_v)]
    early += [(ltaper, ltaper_v), (staper, staper_v)]
    late = [(block, block_v), (value, value_v), (rinv, rinv_v), (horiz, horiz_v), (vert, vert_v)]
    loads = [pltpu.make_async_copy(src, dst, in_sem.at[n]) for n, (src, dst) in enumerate(early + late)]
    for copy in loads[: len(early)]:
        copy.start()

    barrier = pltpu.get_barrier_semaphore()
    greeted = [column_device(r) for r in range(1, PEERS)] + [(left, q), (right, q)]
    greeted += [y_device(k) for k in (1, 2, 3)] + [x_device(k) for k in (1, 2, 3)]
    for device in greeted:
        pl.semaphore_signal(barrier, inc=1, device_id=device, device_id_type=MESH)

    for copy in loads[: len(early)]:
        copy.wait()
    own = pl.ds(ROWS * q, ROWS)
    for i in range(2):
        spart_buf[own, 1 + 2 * h + i] = (sdev_v[:, i] * field_v[:, i]).astype(BF16)
        field_buf[own, 1 + 2 * h + i] = field_v[:, i]
    pl.semaphore_wait(barrier, len(greeted))

    def remote(src, dst, send, recv, where):
        return pltpu.make_async_remote_copy(
            src_ref=src, dst_ref=dst, send_sem=send, recv_sem=recv, device_id=where, device_id_type=MESH
        )

    bufs = (field_buf, spart_buf)

    def f_slot(n, r):
        hr, qr = peer(r)
        return bufs[n].at[pl.ds(ROWS * qr, ROWS), pl.ds(1 + 2 * hr, 2)]

    def f_copy(n, r):
        src = field_v if n == 0 else f_slot(n, 0)
        return remote(src, f_slot(n, 0), f_send.at[n, r], f_recv.at[n, r], column_device(r))

    def f_pass(n, r):
        return remote(f_slot(n, r), f_slot(n, r), f_send.at[n, r + 1], f_recv.at[n, r + 1], column_device(1))

    def f_arrived(n, r):
        remote(f_slot(n, r), f_slot(n, r), f_send.at[n, r], f_recv.at[n, r], column_device(r)).wait_recv()

    def l_copy(r):
        return remote(loc_buf.at[q], loc_buf.at[q], l_send.at[r], l_recv.at[r], column_device(r))

    def l_arrived(r):
        hr, qr = peer(r)
        remote(loc_buf.at[qr], loc_buf.at[qr], l_send.at[r], l_recv.at[r], column_device(r)).wait_recv()

    def e_copy(c, half, r):
        hr, qr = peer(r)
        here = h if half == 0 else 1 - h
        there = 1 + 3 * h if half == 0 else 2 + h
        src = ens.at[pl.ds(OWN * (4 * hr + qr) + PAIR * c, PAIR), :, here]
        dst = ens_buf.at[c, :, pl.ds(ROWS * q, ROWS), there]
        if r == 0:
            return pltpu.make_async_copy(src, dst, es_recv.at[c, half, 0])
        return remote(src, dst, es_send.at[c, half, r], es_recv.at[c, half, r], column_device(r))

    def e_arrived(c, half):
        e_copy(c, half, 0).wait()
        for r in range(1, PEERS):
            hr, qr = peer(r)
            there = 1 + 3 * hr if half == 0 else 2 + hr
            slot = ens_buf.at[c, :, pl.ds(ROWS * qr, ROWS), there]
            remote(slot, slot, es_send.at[c, half, r], es_recv.at[c, half, r], column_device(r)).wait_recv()

    def sides(buf, send, recv, lead):
        mine = [buf.at[lead + (slice(None), 1)], buf.at[lead + (slice(None), 4)]]
        theirs = [buf.at[lead + (slice(None), 5)], buf.at[lead + (slice(None), 0)]]
        return [
            remote(mine[s], theirs[s], send.at[s], recv.at[s], ((left, right)[s], q)) for s in range(2)
        ]

    def e_sides(c):
        return [s for k in range(PAIR) for s in sides(ens_buf, ey_send.at[c, k], ey_recv.at[c, k], (c, k))]

    def f_sides():
        return sides(field_buf, fy_send.at[0], fy_recv.at[0], ()) + sides(
            spart_buf, fy_send.at[1], fy_recv.at[1], ()
        )

    order = (4, 6, 7, 5, 2, 3, 1)
    for n in range(2):
        for r in (4, 6, 2, 1):
            f_copy(n, r).start()
    for r in (2, 3, 1):
        l_copy(r).start()

    def send_members(c, half):
        for r in order:
            e_copy(c, half, r).start()
        e_copy(c, half, 0).start()

    send_members(0, 0)
    for c in range(1, CHUNKS):
        send_members(c, 0)
        send_members(c - 1, 1)
    send_members(CHUNKS - 1, 1)
    for copy in loads[len(early) :]:
        copy.start()

    band(ltaper_v[...], band_e)
    band(staper_v[...], band_s)
    vert_s[...] = spread(svert_v[...])
    vert_e[pl.ds(144 * q, 144)] = spread(loc_buf[q])
    for r in (1, 2, 3):
        l_arrived(r)
        hr, qr = peer(r)
        vert_e[pl.ds(144 * qr, 144)] = spread(loc_buf[qr])
    acc[...] = jnp.zeros_like(acc)

    for n in range(2):
        for r in (2, 6, 4):
            f_arrived(n, r)
            f_pass(n, r).start()
    for n in range(2):
        for r in (1, 3, 7, 5):
            f_arrived(n, r)
    for s in f_sides():
        s.start()
    e_arrived(0, 0)
    for s in e_sides(0):
        s.start()

    for copy in loads[len(early) :]:
        copy.wait()
    slots = block_v.shape[1]
    local = block_v[...] - lon * 16
    pick[...] = ((iota((16, slots), 0) == local) & (block_v[...] >= 0)).astype(F32)
    high, low = halves(horiz_v[...])
    h_cat[:, :128] = high
    h_cat[:, 128:] = low
    high, low = halves(horiz_v[...].T)
    h_turned[:128] = high
    h_turned[128:] = low

    def smooth(weights, read):
        def quad(n, _):
            out_rows = jnp.dot(weights[...], read(4 * n), preferred_element_type=F32).astype(BF16)
            lanes = out_rows.shape[1]
            for ib in range(4):
                zh_buf[ib, pl.ds(pl.multiple_of(32 * n, 32), 32), :lanes] = out_rows[32 * ib : 32 * ib + 32]
            return 0

        lax.fori_loop(0, QUADS, quad, 0, unroll=3)

    def read_static(m):
        return spart_buf[pl.ds(m, 4)].astype(F32).reshape(192, 128).astype(BF16)

    def smooth_members(c):
        def read(m):
            weight = field_buf[pl.ds(m, 4)]
            both = [(ens_buf[c, k, pl.ds(m, 4)].astype(F32) * weight).reshape(192, 128) for k in range(PAIR)]
            return jnp.concatenate(both, axis=1).astype(BF16)

        smooth(band_e, read)

    def mix(c, ib, third):
        rows = pl.ds(pl.multiple_of(192 * third, 192), 192)
        levels = pl.ds(24 * third, 24)
        mixed = jnp.dot(vert_e[rows], zh_buf[ib], preferred_element_type=F32)
        total = acc[ib, levels]
        for k in range(PAIR):
            part = mixed[:, 128 * k : 128 * k + 128].reshape(24, 8, 128)
            total = total + ens_buf[c, k, levels, 1 + ib].astype(F32) * part
        acc[ib, levels] = total
        return 0

    for s in f_sides():
        s.wait()
    smooth(band_s, read_static)
    for i in range(2):
        sv = jnp.dot(vert_s[...], zh_buf[2 * h + i, :, :128], preferred_element_type=F32)
        sv_buf[i] = static_weight * sdev_v[:, i] * sv.reshape(ROWS, 8, 128)

    def chunk(c, _):
        e_arrived(c + 1, 0)
        for s in e_sides(c + 1):
            s.start()
        e_arrived(c, 1)
        for s in e_sides(c):
            s.wait()
        smooth_members(c)
        lax.fori_loop(0, 12, lambda n, _: mix(c, n // 3, n % 3), 0, unroll=3)
        return 0

    last = CHUNKS - 1
    lax.fori_loop(0, last, chunk, 0)

    def tile(n):
        return (2 * (1 - h) + n) % 4

    def d_copy(n, far):
        there = 2 * (1 - zlo if far else zlo) + 1 - core
        src = acc.at[tile(n), pl.ds(ROWS * there, ROWS)]
        return remote(src, d_buf.at[n, far], d_send.at[n, far], d_recv.at[n, far], column_device(1))

    def r_copy(slot, i):
        src = r_out.at[(0, 0, 1)[slot], (0, 1, 1)[slot], i]
        return remote(src, r_buf.at[slot, i], r_send.at[slot, i], r_recv.at[slot, i], column_device((4, 6, 2)[slot]))

    def reduce(n):
        for far in range(2):
            d_copy(n, far).wait_recv()
        for far in range(2):
            if n >= 2 and far == 0:
                continue
            rows = pl.ds(ROWS * (2 * (1 - zlo if far else zlo) + core), ROWS)
            r_out[n // 2, far, n % 2] = (acc[tile(n), rows] + d_buf[n, far]).astype(BF16)
        for slot in (0, 1) if n < 2 else (2,):
            r_copy(slot, n % 2).start()

    e_arrived(last, 1)
    for s in e_sides(last):
        s.wait()
    smooth_members(last)
    for n in range(4):
        lax.fori_loop(0, 3, lambda third, _: mix(last, tile(n), third), 0, unroll=3)
        for far in range(2):
            d_copy(n, far).start()
        if n:
            reduce(n - 1)
    reduce(3)
    for i in range(2):
        total = acc[2 * h + i, own] + d_buf[2 + i, 0]
        for slot in range(3):
            r_copy(slot, i).wait_recv()
            total = total + r_buf[slot, i].astype(F32)
        inc_out[:, i] = ens_weight * total + sv_buf[i]

    cells = swapped(inc_out[...].reshape(36, 8, 128)).reshape(288, 128)
    high, low = halves(cells)
    projected = jnp.dot(jnp.concatenate([high, high], axis=1), h_turned[...], preferred_element_type=F32)
    projected = projected + jnp.dot(low, h_turned[:128], preferred_element_type=F32)
    total = jnp.zeros((16, slots), F32)
    for l in range(ROWS):
        total = total + vert_v[l : l + 1] * projected[16 * l : 16 * l + 16]
    hx_all[q] = jnp.sum(total * pick[...], axis=0, keepdims=True)

    def x_copy(r):
        return remote(hx_all.at[q], hx_all.at[q], x_send.at[r], x_recv.at[r], column_device(r))

    for r in (2, 3, 1):
        x_copy(r).start()
    for r in (1, 2, 3):
        hr, qr = peer(r)
        remote(hx_all.at[qr], hx_all.at[qr], x_send.at[r], x_recv.at[r], column_device(r)).wait_recv()
    miss = hx_all[0] + hx_all[1] + hx_all[2] + hx_all[3] - value_v[...]
    dep = jnp.where(block_v[...] >= 0, rinv_v[...] * miss, 0.0)
    cost = jnp.sum(0.5 * dep * miss, axis=1, keepdims=True)

    def c_copy(phase, k, slot):
        buf, device = ((cost_y, y_device), (cost_x, x_device))[phase]
        return remote(buf.at[slot], buf.at[slot], c_send.at[phase, k], c_recv.at[phase, k], device(k))

    def c_start(phase):
        for k in (2, 1, 3):
            c_copy(phase, k, (py, px)[phase]).start()

    def c_arrived(phase):
        for k in (1, 2, 3):
            c_copy(phase, k, ((py, px)[phase] + 4 - k) % 4).wait_recv()

    def c_last(slot):
        return remote(cost_h.at[slot], cost_h.at[slot], c_send.at[2, 0], c_recv.at[2, 0], column_device(4))

    cost_y[py] = jnp.broadcast_to(cost, (1, 128))
    c_start(0)

    weights = dep * pick[...]
    for l in range(ROWS):
        high, low = halves(vert_v[l : l + 1] * weights)
        spread_hi[16 * l : 16 * l + 16] = high
        spread_lo[16 * l : 16 * l + 16] = low

    c_arrived(0)
    cost_x[px] = cost_y[0] + cost_y[1] + cost_y[2] + cost_y[3]
    c_start(1)

    both = jnp.dot(spread_hi[...], h_cat[...], preferred_element_type=F32)
    adjoint = both[:, :128] + both[:, 128:]
    adjoint = adjoint + jnp.dot(spread_lo[...], h_cat[:, :128], preferred_element_type=F32)
    adj_out[...] = swapped(adjoint.reshape(36, 8, 128)).reshape(ROWS, 2, 8, 128)

    c_arrived(1)
    cost_h[h] = cost_x[0] + cost_x[1] + cost_x[2] + cost_x[3]
    c_last(h).start()

    for n in range(4):
        for far in range(2):
            d_copy(n, far).wait_send()
    for slot in range(3):
        for i in range(2):
            r_copy(slot, i).wait_send()
    for r in (1, 2, 3):
        l_copy(r).wait_send()
        x_copy(r).wait_send()
    for n in range(2):
        for r in (1, 2, 4, 6):
            f_copy(n, r).wait_send()
        for r in (2, 4, 6):
            f_pass(n, r).wait_send()

    def sent(c, _):
        for half in range(2):
            for r in range(1, PEERS):
                e_copy(c, half, r).wait_send()
        return 0

    lax.fori_loop(0, CHUNKS, sent, 0)
    for phase in range(2):
        for k in (1, 2, 3):
            c_copy(phase, k, (py, px)[phase]).wait_send()
    c_last(1 - h).wait_recv()
    cost_out[...] = cost_h[0] + cost_h[1]
    c_last(h).wait_send()


def body(
    field, ens, sdev, lon_taper, static_taper, loc_vert, static_vert, obs_block, obs_value, obs_rinv, obs_horiz, obs_vert
):
    members, slots = ens.shape[0], obs_block.shape[0]
    vmem = pl.BlockSpec(memory_space=pltpu.VMEM)
    hbm = pl.BlockSpec(memory_space=pltpu.HBM)
    dma = pltpu.SemaphoreType.DMA
    tile = (ROWS, 2, 8, 128)
    increment, adjoint, cost = pl.pallas_call(
        kernel,
        out_shape=(
            jax.ShapeDtypeStruct(tile, F32),
            jax.ShapeDtypeStruct(tile, F32),
            jax.ShapeDtypeStruct((1, 128), F32),
        ),
        in_specs=[hbm] * 12,
        out_specs=(vmem, vmem, vmem),
        scratch_shapes=[
            pltpu.VMEM((CHUNKS, PAIR, LEVELS, 6, 8, 128), BF16),
            pltpu.VMEM((LEVELS, 6, 8, 128), F32),
            pltpu.VMEM((LEVELS, 6, 8, 128), BF16),
            pltpu.VMEM((4, ROWS, LEVELS), BF16),
            pltpu.VMEM((4, 576, 256), BF16),
            pltpu.VMEM((128, 192), BF16),
            pltpu.VMEM((128, 192), BF16),
            pltpu.VMEM((576, 576), BF16),
            pltpu.VMEM((144, 576), BF16),
            pltpu.VMEM((4, LEVELS, 8, 128), F32),
            pltpu.VMEM((2, ROWS, 8, 128), F32),
            pltpu.VMEM((4, 2, ROWS, 8, 128), F32),
            pltpu.VMEM((2, 2, 2, ROWS, 8, 128), BF16),
            pltpu.VMEM((3, 2, ROWS, 8, 128), BF16),
            pltpu.VMEM(tile, F32),
            pltpu.VMEM(tile, F32),
            pltpu.VMEM((ROWS, LEVELS), BF16),
            pltpu.VMEM((1, 17), BF16),
            pltpu.VMEM((1, 17), BF16),
            pltpu.VMEM((1, slots), jnp.int32),
            pltpu.VMEM((1, slots), F32),
            pltpu.VMEM((1, slots), F32),
            pltpu.VMEM((slots, 128), F32),
            pltpu.VMEM((ROWS, slots), F32),
            pltpu.VMEM((16, slots), F32),
            pltpu.VMEM((slots, 256), BF16),
            pltpu.VMEM((256, slots), BF16),
            pltpu.VMEM((288, slots), BF16),
            pltpu.VMEM((288, slots), BF16),
            pltpu.VMEM((4, 1, slots), F32),
            pltpu.VMEM((4, 1, 128), F32),
            pltpu.VMEM((4, 1, 128), F32),
            pltpu.VMEM((2, 1, 128), F32),
            dma((CHUNKS, 2, PEERS)),
            dma((CHUNKS, 2, PEERS)),
            dma((CHUNKS, PAIR, 2)),
            dma((CHUNKS, PAIR, 2)),
            dma((2, PEERS)),
            dma((2, PEERS)),
            dma((2, 2)),
            dma((2, 2)),
            dma((4,)),
            dma((4,)),
            dma((4, 2)),
            dma((4, 2)),
            dma((3, 2)),
            dma((3, 2)),
            dma((4,)),
            dma((4,)),
            dma((3, 4)),
            dma((3, 4)),
            dma((11,)),
        ],
        compiler_params=pltpu.CompilerParams(collective_id=0, has_side_effects=True),
        name="members",
    )(
        ens.reshape(members, *tile),
        field.reshape(tile),
        sdev.reshape(tile),
        lon_taper[None],
        static_taper[None],
        loc_vert,
        static_vert,
        obs_block[None],
        obs_value[None],
        obs_rinv[None],
        obs_horiz,
        obs_vert.T,
    )
    return increment.reshape(field.shape), adjoint.reshape(field.shape), cost[0, 0]


def solution(mesh):
    return jax.shard_map(
        body,
        mesh=mesh,
        in_specs=(
            P("lev", "lon", None),
            P(None, "lev", "lon", None),
            P("lev", "lon", None),
            P(),
            P(),
            P("lev", None),
            P("lev", None),
            P("lon"),
            P("lon"),
            P("lon"),
            P("lon", None),
            P("lon", "lev"),
        ),
        out_specs=(P("lev", "lon", None), P("lev", "lon", None), P()),
        check_vma=False,
    )
```

time: 142 us -> 114 us (0.80)
  starting transfers between devices: 10.6 us -> 0 us
  waiting for transfers between devices: 6.53 us -> 0 us
  local copies, waits for them, and re-layouts: 8.46 us -> 3.16 us
  matrix products: 5.02 us -> 0 us
  other arithmetic: 3.1 us -> 0 us
    all_to_all x2 -> x0, starting transfers between devices: 10.6 us -> none  [sent_to_all(): return lax.all_to_all(copies, axis, split_axis=0, concat_axis=0, tiled=True)]
    all_to_all x2 -> x0, waiting for transfers between devices: 6.53 us -> none  [sent_to_all(): return lax.all_to_all(copies, axis, split_axis=0, concat_axis=0, tiled=True)]
    dot_general x2 -> x0, matrix products: 5.02 us -> none  [the longest x1 3.84 us: body(): adj_blocks = jnp.dot(spread, obs_horiz, precision=lax.Precision.HIGHEST)]
    unnamed x22 -> x2, local copies, waits for them, and re-layouts: 5.33 us -> 3.16 us
  transfers between devices with their start and end apart: 2 -> 0, of which waited for: 2 -> 0; matrix products, arithmetic and copies ran while one was open for 4% -> 0% of each run, Pallas kernels for 0% -> 0%
where the time goes in v2:
time: 114 us; the launch traced here: 112 us
  Pallas kernels  106 us (93%)
  local copies, waits for them, and re-layouts  3.16 us (3%)
  between operations  2.46 us (2%)
    pallas_call x1, Pallas kernels, body(): pl.pallas_call(kernel, out_shape=(jax.ShapeDtypeStruct(tile, F32), jax.Sh...  106 us
    unnamed x2, local copies, waits for them, and re-layouts  3.16 us

profile of v2, /device:TPU:1, one launch (start us, length us, event | category | flops | bytes accessed | tf_op | source)
XLA Modules:
  0.0 111.8 jit_solution(9015318465857241630)
XLA Ops:
  0.6 106.2 %members.1 = (f32[18,2,8,128]{3,2,1,0:T(8,128)}, f32[18,2,8,128]{3,2,1,0:T(8,128)}, f32[1,128]{1,0:T(1,128)}) custom-call(bf16[80,18,2,8,128]{4,3,2,1,0:T(8,128)(2,1)} %bitcast.13, f32[18,2,8,128]{3,2,1,0:T(8,128)} %bitcast.14, f32[18,2,8,128]{3,2,1,0:T(8,128)} %bitcast.15, bf16[1,17]{1,0:T(2,128)(2,1)} %bitcast.22, bf16[1,17]{1,0:T(2,128)(2,1)} %bitcast.23, ...), custom_call_target="tpu_custom_call" | custom-call | tf_op jit(solution)/shard_map/members/pallas_call | solution.py:425
  106.9 1.6 %copy.18 = f32[18,16,128]{2,1,0:T(8,128)} copy(f32[18,16,128]{2,1,0:T(8,128)} %bitcast.17) | data formatting | bytes 294912
  108.4 1.6 %copy.19 = f32[18,16,128]{2,1,0:T(8,128)} copy(f32[18,16,128]{2,1,0:T(8,128)} %bitcast.16) | data formatting | bytes 294912

commit v3 on v2

--- a/solution.py
+++ b/solution.py
@@ -16,6 +16,7 @@
 
 COLUMNS = 16
 PEERS = 8
+SECTORS = 32
 CHUNKS = 5
 PAIR = 2
 OWN = CHUNKS * PAIR
@@ -68,9 +69,9 @@
     ens_buf, field_buf, spart_buf, loc_buf, zh_buf, band_e, band_s, vert_e, vert_s, acc, sv_buf,
     d_buf, r_out, r_buf,
     field_v, sdev_v, svert_v, ltaper_v, staper_v, block_v, value_v, rinv_v, horiz_v, vert_v,
-    pick, h_cat, h_turned, spread_hi, spread_lo, hx_all, cost_y, cost_x, cost_h,
+    pick, h_cat, h_turned, spread_hi, spread_lo, hx_all, cost_all,
     es_send, es_recv, ey_send, ey_recv, f_send, f_recv, fy_send, fy_recv, l_send, l_recv,
-    d_send, d_recv, r_send, r_recv, x_send, x_recv, c_send, c_recv, in_sem,
+    d_send, d_recv, r_send, r_recv, x_send, x_recv, c_send, c_recv, in_sem, known,
 ):
     lon, q = lax.axis_index("lon"), lax.axis_index("lev")
     column, h = lon // 2, lon % 2
@@ -127,6 +128,20 @@
         hr, qr = peer(r)
         return bufs[n].at[pl.ds(ROWS * qr, ROWS), pl.ds(1 + 2 * hr, 2)]
 
+    def f_half(n, r, i):
+        hr, qr = peer(r)
+        return bufs[n].at[pl.ds(ROWS * qr, ROWS), 1 + 2 * hr + i]
+
+    def f_relay(n, r):
+        half, sem, to = (0, 4, 2) if r == 6 else (1, 0, 6)
+        slot = f_half(n, r, half)
+        return remote(slot, slot, f_send.at[n, sem], f_recv.at[n, sem], column_device(to))
+
+    def f_relayed(n):
+        for half, sem, via in ((0, 4, 2), (1, 0, 6)):
+            slot = f_half(n, 4, half)
+            remote(slot, slot, f_send.at[n, sem], f_recv.at[n, sem], column_device(via)).wait_recv()
+
     def f_copy(n, r):
         src = field_v if n == 0 else f_slot(n, 0)
         return remote(src, f_slot(n, 0), f_send.at[n, r], f_recv.at[n, r], column_device(r))
@@ -179,7 +194,7 @@
 
     order = (4, 6, 7, 5, 2, 3, 1)
     for n in range(2):
-        for r in (4, 6, 2, 1):
+        for r in (6, 2, 1):
             f_copy(n, r).start()
     for r in (2, 3, 1):
         l_copy(r).start()
@@ -190,15 +205,22 @@
         e_copy(c, half, 0).start()
 
     send_members(0, 0)
+    for k in (1, 2, 3):
+        pl.semaphore_signal(known.at[0], inc=1, device_id=x_device(k), device_id_type=MESH)
+    for copy in loads[len(early) :]:
+        copy.start()
+
+    band(ltaper_v[...], band_e)
+    band(staper_v[...], band_s)
+    for n in range(2):
+        for r in (6, 2):
+            f_arrived(n, r)
+            f_relay(n, r).start()
+            f_pass(n, r).start()
     for c in range(1, CHUNKS):
         send_members(c, 0)
         send_members(c - 1, 1)
     send_members(CHUNKS - 1, 1)
-    for copy in loads[len(early) :]:
-        copy.start()
-
-    band(ltaper_v[...], band_e)
-    band(staper_v[...], band_s)
     vert_s[...] = spread(svert_v[...])
     vert_e[pl.ds(144 * q, 144)] = spread(loc_buf[q])
     for r in (1, 2, 3):
@@ -207,10 +229,13 @@
         vert_e[pl.ds(144 * qr, 144)] = spread(loc_buf[qr])
     acc[...] = jnp.zeros_like(acc)
 
+    pl.semaphore_wait(known.at[0], 3)
+    hr, qr = peer(4)
+    pl.semaphore_signal(known.at[1], inc=1, device_id=(2 * column + hr, qr), device_id_type=MESH)
     for n in range(2):
-        for r in (2, 6, 4):
-            f_arrived(n, r)
-            f_pass(n, r).start()
+        f_relayed(n)
+        f_pass(n, 4).start()
+    pl.semaphore_wait(known.at[1], 1)
     for n in range(2):
         for r in (1, 3, 7, 5):
             f_arrived(n, r)
@@ -347,23 +372,19 @@
     dep = jnp.where(block_v[...] >= 0, rinv_v[...] * miss, 0.0)
     cost = jnp.sum(0.5 * dep * miss, axis=1, keepdims=True)
 
-    def c_copy(phase, k, slot):
-        buf, device = ((cost_y, y_device), (cost_x, x_device))[phase]
-        return remote(buf.at[slot], buf.at[slot], c_send.at[phase, k], c_recv.at[phase, k], device(k))
-
-    def c_start(phase):
-        for k in (2, 1, 3):
-            c_copy(phase, k, (py, px)[phase]).start()
-
-    def c_arrived(phase):
-        for k in (1, 2, 3):
-            c_copy(phase, k, ((py, px)[phase] + 4 - k) % 4).wait_recv()
-
-    def c_last(slot):
-        return remote(cost_h.at[slot], cost_h.at[slot], c_send.at[2, 0], c_recv.at[2, 0], column_device(4))
-
-    cost_y[py] = jnp.broadcast_to(cost, (1, 128))
-    c_start(0)
+    def c_copy(k, slot):
+        where = ((lon + k) % SECTORS, q)
+        return remote(cost_all.at[slot], cost_all.at[slot], c_send.at[k], c_recv.at[k], where)
+
+    def c_each(act):
+        def one(k, _):
+            act(k)
+            return 0
+
+        lax.fori_loop(1, SECTORS, one, 0)
+
+    cost_all[lon] = jnp.broadcast_to(cost, (1, 128))
+    c_each(lambda k: c_copy(k, lon).start())
 
     weights = dep * pick[...]
     for l in range(ROWS):
@@ -371,18 +392,12 @@
         spread_hi[16 * l : 16 * l + 16] = high
         spread_lo[16 * l : 16 * l + 16] = low
 
-    c_arrived(0)
-    cost_x[px] = cost_y[0] + cost_y[1] + cost_y[2] + cost_y[3]
-    c_start(1)
 
     both = jnp.dot(spread_hi[...], h_cat[...], preferred_element_type=F32)
     adjoint = both[:, :128] + both[:, 128:]
     adjoint = adjoint + jnp.dot(spread_lo[...], h_cat[:, :128], preferred_element_type=F32)
     adj_out[...] = swapped(adjoint.reshape(36, 8, 128)).reshape(ROWS, 2, 8, 128)
 
-    c_arrived(1)
-    cost_h[h] = cost_x[0] + cost_x[1] + cost_x[2] + cost_x[3]
-    c_last(h).start()
 
     for n in range(4):
         for far in range(2):
@@ -394,8 +409,10 @@
         l_copy(r).wait_send()
         x_copy(r).wait_send()
     for n in range(2):
-        for r in (1, 2, 4, 6):
+        for r in (1, 2, 6):
             f_copy(n, r).wait_send()
+        for r in (2, 6):
+            f_relay(n, r).wait_send()
         for r in (2, 4, 6):
             f_pass(n, r).wait_send()
 
@@ -406,12 +423,9 @@
         return 0
 
     lax.fori_loop(0, CHUNKS, sent, 0)
-    for phase in range(2):
-        for k in (1, 2, 3):
-            c_copy(phase, k, (py, px)[phase]).wait_send()
-    c_last(1 - h).wait_recv()
-    cost_out[...] = cost_h[0] + cost_h[1]
-    c_last(h).wait_send()
+    c_each(lambda k: c_copy(k, lon).wait_send())
+    c_each(lambda k: c_copy(k, (lon + SECTORS - k) % SECTORS).wait_recv())
+    cost_out[...] = jnp.sum(cost_all[...], axis=0)
 
 
 def body(
@@ -462,9 +476,7 @@
             pltpu.VMEM((288, slots), BF16),
             pltpu.VMEM((288, slots), BF16),
             pltpu.VMEM((4, 1, slots), F32),
-            pltpu.VMEM((4, 1, 128), F32),
-            pltpu.VMEM((4, 1, 128), F32),
-            pltpu.VMEM((2, 1, 128), F32),
+            pltpu.VMEM((SECTORS, 1, 128), F32),
             dma((CHUNKS, 2, PEERS)),
             dma((CHUNKS, 2, PEERS)),
             dma((CHUNKS, PAIR, 2)),
@@ -481,25 +493,31 @@
             dma((3, 2)),
             dma((4,)),
             dma((4,)),
-            dma((3, 4)),
-            dma((3, 4)),
+            dma((SECTORS,)),
+            dma((SECTORS,)),
             dma((11,)),
+            pltpu.SemaphoreType.REGULAR((2,)),
         ],
-        compiler_params=pltpu.CompilerParams(collective_id=0, has_side_effects=True),
+        compiler_params=pltpu.CompilerParams(collective_id=0, has_side_effects=True, vmem_limit_bytes=48 * 1024 * 1024),
         name="members",
     )(
-        ens.reshape(members, *tile),
-        field.reshape(tile),
-        sdev.reshape(tile),
-        lon_taper[None],
-        static_taper[None],
-        loc_vert,
-        static_vert,
-        obs_block[None],
-        obs_value[None],
-        obs_rinv[None],
-        obs_horiz,
-        obs_vert.T,
+        *(
+            pltpu.with_memory_space_constraint(x, pltpu.HBM)
+            for x in (
+                ens.reshape(members, *tile),
+                field.reshape(tile),
+                sdev.reshape(tile),
+                lon_taper[None],
+                static_taper[None],
+                loc_vert,
+                static_vert,
+                obs_block[None],
+                obs_value[None],
+                obs_rinv[None],
+                obs_horiz,
+                obs_vert.T,
+            )
+        )
     )
     return increment.reshape(field.shape), adjoint.reshape(field.shape), cost[0, 0]
 

time: 114 us -> 105 us (0.921); the launches traced: 112 us -> 104 us
  Pallas kernels: 106 us -> 101 us
  local copies, waits for them, and re-layouts: 3.16 us -> 1.32 us
    pallas_call x1, Pallas kernels: 106 us -> 101 us  [body(): pl.pallas_call(kernel, out_shape=(jax.ShapeDtypeStruct(tile, F32), jax.Sh...]
    unnamed x2, local copies, waits for them, and re-layouts: 3.16 us -> 1.32 us
where the time goes in v3:
time: 105 us; the launch traced here: 104 us
  Pallas kernels  101 us (96%)
  between operations  1.81 us (2%)
  local copies, waits for them, and re-layouts  1.32 us (1%)
    pallas_call x1, Pallas kernels, body(): pl.pallas_call(kernel, out_shape=(jax.ShapeDtypeStruct(tile, F32), jax.Sh...  101 us

profile of v3, /device:TPU:1, one launch (start us, length us, event | category | flops | bytes accessed | tf_op | source)
XLA Modules:
  0.0 104.4 jit_solution(11716480755559036378)
XLA Ops:
  0.6 101.2 %members.1 = (f32[18,2,8,128]{3,2,1,0:T(8,128)S(1)}, f32[18,2,8,128]{3,2,1,0:T(8,128)S(1)}, f32[1,128]{1,0:T(1,128)S(1)}) custom-call(bf16[80,18,2,8,128]{4,3,2,1,0:T(8,128)(2,1)} %bitcast.16, f32[18,2,8,128]{3,2,1,0:T(8,128)} %bitcast.17, f32[18,2,8,128]{3,2,1,0:T(8,128)} %bitcast.18, bf16[1,17]{1,0:T(2,128)(2,1)} %bitcast.23, bf16[1,17]{1,0:T(2,128)(2,1)} %bitcast.24, ...), custom_call_target="tpu_custom_call" | custom-call | tf_op jit(solution)/shard_map/members/pallas_call | solution.py:439
  101.9 0.7 copy.18
  102.6 0.7 copy.19

commit v4 on v3

--- a/solution.py
+++ b/solution.py
@@ -56,6 +56,11 @@
         before = after if b == 4 else pltpu.roll(pltpu.roll(x, b, 1), 128 - 16 * b, 2)
         x = jnp.where(row_bit == group_bit, x, jnp.where(row_bit == 0, after, before))
     return x
+
+
+def far_away(k):
+    x, y, z = k // 8, (k // 2) % 4, k % 2
+    return min(x, 4 - x) + min(y, 4 - y) + 2 * z
 
 
 def halves(x):
@@ -159,23 +164,30 @@
         hr, qr = peer(r)
         remote(loc_buf.at[qr], loc_buf.at[qr], l_send.at[r], l_recv.at[r], column_device(r)).wait_recv()
 
-    def e_copy(c, half, r):
+    def piece(n, half):
+        if isinstance(n, int) and half == 1 and n >= CHUNKS - 1:
+            return OWN - 2 + n - (CHUNKS - 1), 1
+        return PAIR * n, PAIR
+
+    def e_copy(n, half, r):
         hr, qr = peer(r)
+        first, count = piece(n, half)
         here = h if half == 0 else 1 - h
         there = 1 + 3 * h if half == 0 else 2 + h
-        src = ens.at[pl.ds(OWN * (4 * hr + qr) + PAIR * c, PAIR), :, here]
-        dst = ens_buf.at[c, :, pl.ds(ROWS * q, ROWS), there]
+        src = ens.at[pl.ds(OWN * (4 * hr + qr) + first, count), :, here]
+        dst = ens_buf.at[pl.ds(first, count), pl.ds(ROWS * q, ROWS), there]
         if r == 0:
-            return pltpu.make_async_copy(src, dst, es_recv.at[c, half, 0])
-        return remote(src, dst, es_send.at[c, half, r], es_recv.at[c, half, r], column_device(r))
-
-    def e_arrived(c, half):
-        e_copy(c, half, 0).wait()
+            return pltpu.make_async_copy(src, dst, es_recv.at[n, half, 0])
+        return remote(src, dst, es_send.at[n, half, r], es_recv.at[n, half, r], column_device(r))
+
+    def e_arrived(n, half):
+        first, count = piece(n, half)
+        e_copy(n, half, 0).wait()
         for r in range(1, PEERS):
             hr, qr = peer(r)
             there = 1 + 3 * hr if half == 0 else 2 + hr
-            slot = ens_buf.at[c, :, pl.ds(ROWS * qr, ROWS), there]
-            remote(slot, slot, es_send.at[c, half, r], es_recv.at[c, half, r], column_device(r)).wait_recv()
+            slot = ens_buf.at[pl.ds(first, count), pl.ds(ROWS * qr, ROWS), there]
+            remote(slot, slot, es_send.at[n, half, r], es_recv.at[n, half, r], column_device(r)).wait_recv()
 
     def sides(buf, send, recv, lead):
         mine = [buf.at[lead + (slice(None), 1)], buf.at[lead + (slice(None), 4)]]
@@ -185,7 +197,7 @@
         ]
 
     def e_sides(c):
-        return [s for k in range(PAIR) for s in sides(ens_buf, ey_send.at[c, k], ey_recv.at[c, k], (c, k))]
+        return [s for k in range(PAIR) for s in sides(ens_buf, ey_send.at[c, k], ey_recv.at[c, k], (PAIR * c + k,))]
 
     def f_sides():
         return sides(field_buf, fy_send.at[0], fy_recv.at[0], ()) + sides(
@@ -221,6 +233,7 @@
         send_members(c, 0)
         send_members(c - 1, 1)
     send_members(CHUNKS - 1, 1)
+    send_members(CHUNKS, 1)
     vert_s[...] = spread(svert_v[...])
     vert_e[pl.ds(144 * q, 144)] = spread(loc_buf[q])
     for r in (1, 2, 3):
@@ -273,7 +286,7 @@
     def smooth_members(c):
         def read(m):
             weight = field_buf[pl.ds(m, 4)]
-            both = [(ens_buf[c, k, pl.ds(m, 4)].astype(F32) * weight).reshape(192, 128) for k in range(PAIR)]
+            both = [(ens_buf[PAIR * c + k, pl.ds(m, 4)].astype(F32) * weight).reshape(192, 128) for k in range(PAIR)]
             return jnp.concatenate(both, axis=1).astype(BF16)
 
         smooth(band_e, read)
@@ -285,8 +298,35 @@
         total = acc[ib, levels]
         for k in range(PAIR):
             part = mixed[:, 128 * k : 128 * k + 128].reshape(24, 8, 128)
-            total = total + ens_buf[c, k, levels, 1 + ib].astype(F32) * part
+            total = total + ens_buf[PAIR * c + k, levels, 1 + ib].astype(F32) * part
         acc[ib, levels] = total
+        return 0
+
+    def smooth_one(k):
+        def pair_of_quads(n, _):
+            both = [
+                (ens_buf[k, pl.ds(8 * n + 4 * g, 4)].astype(F32) * field_buf[pl.ds(8 * n + 4 * g, 4)]).reshape(192, 128)
+                for g in range(2)
+            ]
+            rows = jnp.concatenate(both, axis=1).astype(BF16)
+            out_rows = jnp.dot(band_e[...], rows, preferred_element_type=F32).astype(BF16)
+            for ib in range(4):
+                lanes = slice(128 * (ib % 2), 128 * (ib % 2) + 128)
+                for g in range(2):
+                    at = pl.ds(pl.multiple_of(64 * n + 32 * g, 32), 32)
+                    zh_buf[ib // 2, at, lanes] = out_rows[32 * ib : 32 * ib + 32, 128 * g : 128 * g + 128]
+            return 0
+
+        lax.fori_loop(0, QUADS // 2, pair_of_quads, 0, unroll=3)
+
+    def mix_one(k, side, third):
+        rows = pl.ds(pl.multiple_of(192 * third, 192), 192)
+        levels = pl.ds(24 * third, 24)
+        mixed = jnp.dot(vert_e[rows], zh_buf[side], preferred_element_type=F32)
+        for i in range(2):
+            part = mixed[:, 128 * i : 128 * i + 128].reshape(24, 8, 128)
+            tile_at = 2 * side + i
+            acc[tile_at, levels] = acc[tile_at, levels] + ens_buf[k, levels, 1 + tile_at].astype(F32) * part
         return 0
 
     for s in f_sides():
@@ -304,7 +344,7 @@
         for s in e_sides(c):
             s.wait()
         smooth_members(c)
-        lax.fori_loop(0, 12, lambda n, _: mix(c, n // 3, n % 3), 0, unroll=3)
+        lax.fori_loop(0, 12, lambda n, _: mix(c, n // 3, n % 3), 0, unroll=6)
         return 0
 
     last = CHUNKS - 1
@@ -336,13 +376,20 @@
     e_arrived(last, 1)
     for s in e_sides(last):
         s.wait()
-    smooth_members(last)
-    for n in range(4):
-        lax.fori_loop(0, 3, lambda third, _: mix(last, tile(n), third), 0, unroll=3)
-        for far in range(2):
-            d_copy(n, far).start()
-        if n:
-            reduce(n - 1)
+    smooth_one(OWN - 2)
+    lax.fori_loop(0, 6, lambda n, _: mix_one(OWN - 2, n // 3, n % 3), 0, unroll=6)
+    e_arrived(last + 1, 1)
+    smooth_one(OWN - 1)
+    for turn in range(2):
+        side = 1 - h if turn == 0 else h
+        lax.fori_loop(0, 3, lambda third, _: mix_one(OWN - 1, side, third), 0, unroll=3)
+        for n in (2 * turn, 2 * turn + 1):
+            for far in range(2):
+                d_copy(n, far).start()
+        if turn:
+            reduce(0)
+            reduce(1)
+    reduce(2)
     reduce(3)
     for i in range(2):
         total = acc[2 * h + i, own] + d_buf[2 + i, 0]
@@ -373,7 +420,8 @@
     cost = jnp.sum(0.5 * dep * miss, axis=1, keepdims=True)
 
     def c_copy(k, slot):
-        where = ((lon + k) % SECTORS, q)
+        other = lon + k
+        where = (jnp.where(other >= SECTORS, other - SECTORS, other), q)
         return remote(cost_all.at[slot], cost_all.at[slot], c_send.at[k], c_recv.at[k], where)
 
     def c_each(act):
@@ -384,7 +432,8 @@
         lax.fori_loop(1, SECTORS, one, 0)
 
     cost_all[lon] = jnp.broadcast_to(cost, (1, 128))
-    c_each(lambda k: c_copy(k, lon).start())
+    for k in sorted(range(1, SECTORS), key=lambda k: -far_away(k)):
+        c_copy(k, lon).start()
 
     weights = dep * pick[...]
     for l in range(ROWS):
@@ -422,10 +471,25 @@
                 e_copy(c, half, r).wait_send()
         return 0
 
-    lax.fori_loop(0, CHUNKS, sent, 0)
+    lax.fori_loop(0, CHUNKS - 1, sent, 0)
+    for r in range(1, PEERS):
+        e_copy(CHUNKS - 1, 0, r).wait_send()
+        e_copy(CHUNKS - 1, 1, r).wait_send()
+        e_copy(CHUNKS, 1, r).wait_send()
     c_each(lambda k: c_copy(k, lon).wait_send())
     c_each(lambda k: c_copy(k, (lon + SECTORS - k) % SECTORS).wait_recv())
     cost_out[...] = jnp.sum(cost_all[...], axis=0)
+
+
+def deliver(inc, adj, cost, inc_out, adj_out, cost_out, sem):
+    copies = [
+        pltpu.make_async_copy(src, dst, sem.at[n])
+        for n, (src, dst) in enumerate(((inc, inc_out), (adj, adj_out), (cost, cost_out)))
+    ]
+    for copy in copies:
+        copy.start()
+    for copy in copies:
+        copy.wait()
 
 
 def body(
@@ -446,7 +510,7 @@
         in_specs=[hbm] * 12,
         out_specs=(vmem, vmem, vmem),
         scratch_shapes=[
-            pltpu.VMEM((CHUNKS, PAIR, LEVELS, 6, 8, 128), BF16),
+            pltpu.VMEM((OWN, LEVELS, 6, 8, 128), BF16),
             pltpu.VMEM((LEVELS, 6, 8, 128), F32),
             pltpu.VMEM((LEVELS, 6, 8, 128), BF16),
             pltpu.VMEM((4, ROWS, LEVELS), BF16),
@@ -477,8 +541,8 @@
             pltpu.VMEM((288, slots), BF16),
             pltpu.VMEM((4, 1, slots), F32),
             pltpu.VMEM((SECTORS, 1, 128), F32),
-            dma((CHUNKS, 2, PEERS)),
-            dma((CHUNKS, 2, PEERS)),
+            dma((CHUNKS + 1, 2, PEERS)),
+            dma((CHUNKS + 1, 2, PEERS)),
             dma((CHUNKS, PAIR, 2)),
             dma((CHUNKS, PAIR, 2)),
             dma((2, PEERS)),
@@ -519,6 +583,16 @@
             )
         )
     )
+    shapes = [jax.ShapeDtypeStruct(x.shape, F32) for x in (increment, adjoint, cost)]
+    increment, adjoint, cost = pl.pallas_call(
+        deliver,
+        out_shape=shapes,
+        in_specs=[vmem] * 3,
+        out_specs=[hbm] * 3,
+        scratch_shapes=[dma((3,))],
+        compiler_params=pltpu.CompilerParams(vmem_limit_bytes=4 * 1024 * 1024),
+        name="deliver",
+    )(increment, adjoint, cost)
     return increment.reshape(field.shape), adjoint.reshape(field.shape), cost[0, 0]
 
 

time: 105 us -> 102 us (0.971)
  local copies, waits for them, and re-layouts: 1.32 us -> 0 us
  between operations: 1.81 us -> 0.64 us
    unnamed x2 -> x0, local copies, waits for them, and re-layouts: 1.32 us -> none
where the time goes in v4:
time: 102 us
  Pallas kernels  102 us (100%)
    pallas_call x1, Pallas kernels, body(): pl.pallas_call(kernel, out_shape=(jax.ShapeDtypeStruct(tile, F32), jax.Sh...  101 us

profile of v4, /device:TPU:1, one launch (start us, length us, event | category | flops | bytes accessed | tf_op | source)
XLA Modules:
  0.0 102.2 jit_solution(7136045382613162452)
XLA Ops:
  0.6 100.8 %members.1 = (f32[18,2,8,128]{3,2,1,0:T(8,128)S(1)}, f32[18,2,8,128]{3,2,1,0:T(8,128)S(1)}, f32[1,128]{1,0:T(1,128)S(1)}) custom-call(bf16[80,18,2,8,128]{4,3,2,1,0:T(8,128)(2,1)} %bitcast.13, f32[18,2,8,128]{3,2,1,0:T(8,128)} %bitcast.14, f32[18,2,8,128]{3,2,1,0:T(8,128)} %bitcast.15, bf16[1,17]{1,0:T(2,128)(2,1)} %bitcast.20, bf16[1,17]{1,0:T(2,128)(2,1)} %bitcast.21, ...), custom_call_target="tpu_custom_call" | custom-call | tf_op jit(solution)/shard_map/members/pallas_call | solution.py:503
  101.4 0.7 deliver.1

commit v5 on v4

--- a/solution.py
+++ b/solution.py
@@ -105,15 +105,14 @@
     early += [(ltaper, ltaper_v), (staper, staper_v)]
     late = [(block, block_v), (value, value_v), (rinv, rinv_v), (horiz, horiz_v), (vert, vert_v)]
     loads = [pltpu.make_async_copy(src, dst, in_sem.at[n]) for n, (src, dst) in enumerate(early + late)]
-    for copy in loads[: len(early)]:
-        copy.start()
-
     barrier = pltpu.get_barrier_semaphore()
     greeted = [column_device(r) for r in range(1, PEERS)] + [(left, q), (right, q)]
     greeted += [y_device(k) for k in (1, 2, 3)] + [x_device(k) for k in (1, 2, 3)]
     for device in greeted:
         pl.semaphore_signal(barrier, inc=1, device_id=device, device_id_type=MESH)
 
+    for copy in loads[: len(early)]:
+        copy.start()
     for copy in loads[: len(early)]:
         copy.wait()
     own = pl.ds(ROWS * q, ROWS)
@@ -204,7 +203,7 @@
             spart_buf, fy_send.at[1], fy_recv.at[1], ()
         )
 
-    order = (4, 6, 7, 5, 2, 3, 1)
+    order = (2, 6, 4, 3, 7, 5, 1)
     for n in range(2):
         for r in (6, 2, 1):
             f_copy(n, r).start()
@@ -278,7 +277,7 @@
                 zh_buf[ib, pl.ds(pl.multiple_of(32 * n, 32), 32), :lanes] = out_rows[32 * ib : 32 * ib + 32]
             return 0
 
-        lax.fori_loop(0, QUADS, quad, 0, unroll=3)
+        lax.fori_loop(0, QUADS, quad, 0, unroll=9)
 
     def read_static(m):
         return spart_buf[pl.ds(m, 4)].astype(F32).reshape(192, 128).astype(BF16)
@@ -317,7 +316,7 @@
                     zh_buf[ib // 2, at, lanes] = out_rows[32 * ib : 32 * ib + 32, 128 * g : 128 * g + 128]
             return 0
 
-        lax.fori_loop(0, QUADS // 2, pair_of_quads, 0, unroll=3)
+        lax.fori_loop(0, QUADS // 2, pair_of_quads, 0, unroll=9)
 
     def mix_one(k, side, third):
         rows = pl.ds(pl.multiple_of(192 * third, 192), 192)
@@ -344,7 +343,7 @@
         for s in e_sides(c):
             s.wait()
         smooth_members(c)
-        lax.fori_loop(0, 12, lambda n, _: mix(c, n // 3, n % 3), 0, unroll=6)
+        lax.fori_loop(0, 12, lambda n, _: mix(c, n // 3, n % 3), 0, unroll=12)
         return 0
 
     last = CHUNKS - 1

time: 102 us -> 101 us (level)
  no operation moved by 1% of the time
where the time goes in v5:
time: 101 us
  Pallas kernels  101 us (100%)
    pallas_call x1, Pallas kernels, body(): pl.pallas_call(kernel, out_shape=(jax.ShapeDtypeStruct(tile, F32), jax.Sh...  99.9 us

profile of v5, /device:TPU:1, one launch (start us, length us, event | category | flops | bytes accessed | tf_op | source)
XLA Modules:
  0.0 101.3 jit_solution(14826249389826728764)
XLA Ops:
  0.6 99.9 %members.1 = (f32[18,2,8,128]{3,2,1,0:T(8,128)S(1)}, f32[18,2,8,128]{3,2,1,0:T(8,128)S(1)}, f32[1,128]{1,0:T(1,128)S(1)}) custom-call(bf16[80,18,2,8,128]{4,3,2,1,0:T(8,128)(2,1)} %bitcast.13, f32[18,2,8,128]{3,2,1,0:T(8,128)} %bitcast.14, f32[18,2,8,128]{3,2,1,0:T(8,128)} %bitcast.15, bf16[1,17]{1,0:T(2,128)(2,1)} %bitcast.20, bf16[1,17]{1,0:T(2,128)(2,1)} %bitcast.21, ...), custom_call_target="tpu_custom_call" | custom-call | tf_op jit(solution)/shard_map/members/pallas_call | solution.py:502
  100.6 0.7 deliver.1

commit v6 on v5

--- a/solution.py
+++ b/solution.py
@@ -17,9 +17,9 @@
 COLUMNS = 16
 PEERS = 8
 SECTORS = 32
-CHUNKS = 5
+GROUPS = (((0, 4), (4, 4), (8, 2)), ((0, 4), (4, 4), (8, 1), (9, 1)))
 PAIR = 2
-OWN = CHUNKS * PAIR
+OWN = 10
 LEVELS = 72
 ROWS = 18
 QUADS = LEVELS // 4
@@ -163,14 +163,9 @@
         hr, qr = peer(r)
         remote(loc_buf.at[qr], loc_buf.at[qr], l_send.at[r], l_recv.at[r], column_device(r)).wait_recv()
 
-    def piece(n, half):
-        if isinstance(n, int) and half == 1 and n >= CHUNKS - 1:
-            return OWN - 2 + n - (CHUNKS - 1), 1
-        return PAIR * n, PAIR
-
     def e_copy(n, half, r):
         hr, qr = peer(r)
-        first, count = piece(n, half)
+        first, count = GROUPS[half][n]
         here = h if half == 0 else 1 - h
         there = 1 + 3 * h if half == 0 else 2 + h
         src = ens.at[pl.ds(OWN * (4 * hr + qr) + first, count), :, here]
@@ -180,7 +175,7 @@
         return remote(src, dst, es_send.at[n, half, r], es_recv.at[n, half, r], column_device(r))
 
     def e_arrived(n, half):
-        first, count = piece(n, half)
+        first, count = GROUPS[half][n]
         e_copy(n, half, 0).wait()
         for r in range(1, PEERS):
             hr, qr = peer(r)
@@ -196,7 +191,9 @@
         ]
 
     def e_sides(c):
-        return [s for k in range(PAIR) for s in sides(ens_buf, ey_send.at[c, k], ey_recv.at[c, k], (PAIR * c + k,))]
+        first, count = GROUPS[0][c]
+        members = range(first, first + count)
+        return [s for k in members for s in sides(ens_buf, ey_send.at[k], ey_recv.at[k], (k,))]
 
     def f_sides():
         return sides(field_buf, fy_send.at[0], fy_recv.at[0], ()) + sides(
@@ -228,11 +225,11 @@
             f_arrived(n, r)
             f_relay(n, r).start()
             f_pass(n, r).start()
-    for c in range(1, CHUNKS):
-        send_members(c, 0)
-        send_members(c - 1, 1)
-    send_members(CHUNKS - 1, 1)
-    send_members(CHUNKS, 1)
+    send_members(1, 0)
+    send_members(0, 1)
+    send_members(2, 0)
+    for c in (1, 2, 3):
+        send_members(c, 1)
     vert_s[...] = spread(svert_v[...])
     vert_e[pl.ds(144 * q, 144)] = spread(loc_buf[q])
     for r in (1, 2, 3):
@@ -335,19 +332,19 @@
         sv = jnp.dot(vert_s[...], zh_buf[2 * h + i, :, :128], preferred_element_type=F32)
         sv_buf[i] = static_weight * sdev_v[:, i] * sv.reshape(ROWS, 8, 128)
 
-    def chunk(c, _):
-        e_arrived(c + 1, 0)
-        for s in e_sides(c + 1):
-            s.start()
-        e_arrived(c, 1)
-        for s in e_sides(c):
-            s.wait()
+    def pair(c, _):
         smooth_members(c)
         lax.fori_loop(0, 12, lambda n, _: mix(c, n // 3, n % 3), 0, unroll=12)
         return 0
 
-    last = CHUNKS - 1
-    lax.fori_loop(0, last, chunk, 0)
+    for g in range(2):
+        e_arrived(g + 1, 0)
+        for s in e_sides(g + 1):
+            s.start()
+        e_arrived(g, 1)
+        for s in e_sides(g):
+            s.wait()
+        lax.fori_loop(2 * g, 2 * g + 2, pair, 0)
 
     def tile(n):
         return (2 * (1 - h) + n) % 4
@@ -372,12 +369,12 @@
         for slot in (0, 1) if n < 2 else (2,):
             r_copy(slot, n % 2).start()
 
-    e_arrived(last, 1)
-    for s in e_sides(last):
+    e_arrived(2, 1)
+    for s in e_sides(2):
         s.wait()
     smooth_one(OWN - 2)
     lax.fori_loop(0, 6, lambda n, _: mix_one(OWN - 2, n // 3, n % 3), 0, unroll=6)
-    e_arrived(last + 1, 1)
+    e_arrived(3, 1)
     smooth_one(OWN - 1)
     for turn in range(2):
         side = 1 - h if turn == 0 else h
@@ -464,17 +461,10 @@
         for r in (2, 4, 6):
             f_pass(n, r).wait_send()
 
-    def sent(c, _):
-        for half in range(2):
+    for half in range(2):
+        for n in range(len(GROUPS[half])):
             for r in range(1, PEERS):
-                e_copy(c, half, r).wait_send()
-        return 0
-
-    lax.fori_loop(0, CHUNKS - 1, sent, 0)
-    for r in range(1, PEERS):
-        e_copy(CHUNKS - 1, 0, r).wait_send()
-        e_copy(CHUNKS - 1, 1, r).wait_send()
-        e_copy(CHUNKS, 1, r).wait_send()
+                e_copy(n, half, r).wait_send()
     c_each(lambda k: c_copy(k, lon).wait_send())
     c_each(lambda k: c_copy(k, (lon + SECTORS - k) % SECTORS).wait_recv())
     cost_out[...] = jnp.sum(cost_all[...], axis=0)
@@ -540,10 +530,10 @@
             pltpu.VMEM((288, slots), BF16),
             pltpu.VMEM((4, 1, slots), F32),
             pltpu.VMEM((SECTORS, 1, 128), F32),
-            dma((CHUNKS + 1, 2, PEERS)),
-            dma((CHUNKS + 1, 2, PEERS)),
-            dma((CHUNKS, PAIR, 2)),
-            dma((CHUNKS, PAIR, 2)),
+            dma((4, 2, PEERS)),
+            dma((4, 2, PEERS)),
+            dma((OWN, 2)),
+            dma((OWN, 2)),
             dma((2, PEERS)),
             dma((2, PEERS)),
             dma((2, 2)),

time: 101 us -> 101 us (level)
  no operation moved by 1% of the time
where the time goes in v6:
time: 101 us
  Pallas kernels  100 us (99%)
    pallas_call x1, Pallas kernels, body(): pl.pallas_call(kernel, out_shape=(jax.ShapeDtypeStruct(tile, F32), jax.Sh...  99.7 us

profile of v6, /device:TPU:1, one launch (start us, length us, event | category | flops | bytes accessed | tf_op | source)
XLA Modules:
  0.0 101.1 jit_solution(16983960878487907070)
XLA Ops:
  0.6 99.7 %members.1 = (f32[18,2,8,128]{3,2,1,0:T(8,128)S(1)}, f32[18,2,8,128]{3,2,1,0:T(8,128)S(1)}, f32[1,128]{1,0:T(1,128)S(1)}) custom-call(bf16[80,18,2,8,128]{4,3,2,1,0:T(8,128)(2,1)} %bitcast.13, f32[18,2,8,128]{3,2,1,0:T(8,128)} %bitcast.14, f32[18,2,8,128]{3,2,1,0:T(8,128)} %bitcast.15, bf16[1,17]{1,0:T(2,128)(2,1)} %bitcast.20, bf16[1,17]{1,0:T(2,128)(2,1)} %bitcast.21, ...), custom_call_target="tpu_custom_call" | custom-call | tf_op jit(solution)/shard_map/members/pallas_call | solution.py:492
  100.3 0.7 deliver.1

commit v7 on v5

--- a/solution.py
+++ b/solution.py
@@ -476,7 +476,8 @@
         e_copy(CHUNKS - 1, 1, r).wait_send()
         e_copy(CHUNKS, 1, r).wait_send()
     c_each(lambda k: c_copy(k, lon).wait_send())
-    c_each(lambda k: c_copy(k, (lon + SECTORS - k) % SECTORS).wait_recv())
+    for k in sorted(range(1, SECTORS), key=far_away):
+        c_copy(k, jnp.where(lon >= k, lon - k, lon + SECTORS - k)).wait_recv()
     cost_out[...] = jnp.sum(cost_all[...], axis=0)
 
 

time: 101 us -> 101 us (level)
  no operation moved by 1% of the time
where the time goes in v7:
time: 101 us
  Pallas kernels  101 us (100%)
    pallas_call x1, Pallas kernels, body(): pl.pallas_call(kernel, out_shape=(jax.ShapeDtypeStruct(tile, F32), jax.Sh...  99.9 us

profile of v7, /device:TPU:1, one launch (start us, length us, event | category | flops | bytes accessed | tf_op | source)
XLA Modules:
  0.0 101.2 jit_solution(14051784872798791698)
XLA Ops:
  0.6 99.9 %members.1 = (f32[18,2,8,128]{3,2,1,0:T(8,128)S(1)}, f32[18,2,8,128]{3,2,1,0:T(8,128)S(1)}, f32[1,128]{1,0:T(1,128)S(1)}) custom-call(bf16[80,18,2,8,128]{4,3,2,1,0:T(8,128)(2,1)} %bitcast.13, f32[18,2,8,128]{3,2,1,0:T(8,128)} %bitcast.14, f32[18,2,8,128]{3,2,1,0:T(8,128)} %bitcast.15, bf16[1,17]{1,0:T(2,128)(2,1)} %bitcast.20, bf16[1,17]{1,0:T(2,128)(2,1)} %bitcast.21, ...), custom_call_target="tpu_custom_call" | custom-call | tf_op jit(solution)/shard_map/members/pallas_call | solution.py:503
  100.5 0.7 deliver.1
